TPU v7x, 128 devices: a whole 4x4x4 slice. The times are simulated.
128 devices in a mesh: grp: 2 (over x_lo), blk: 64 (over y, x_hi, z, core).
Axes of the slice: x: 4 (x_hi: 2, x_lo: 2; x = x_hi * 2 + x_lo), y: 4, z: 4, core: 2. Of those that a mesh axis runs over, the one named last changes fastest.
Arguments:
- zonal_velocity_field: bfloat16 [2048, 64, 128], P('blk'), may hold values from -6 to 6
- meridional_velocity_field: bfloat16 [2048, 64, 128], P('blk'), may hold values from -6 to 6
- barometric_disturbance: bfloat16 [2048, 64, 128], P('blk'), may hold values from -6 to 6
- delayed_thermal_deviation: bfloat16 [2048, 64, 128], P('blk'), may hold values from -6 to 6
- delayed_moisture_deviation: bfloat16 [2048, 64, 128], P('blk'), may hold values from -6 to 6
- flow_category_label: int32 [2048, 64], P('blk'), may hold values from 0 to 63, as said below
- advective_stability_number: float32 [128], replicated, may hold values from 0.25 to 1.3
- initial_dense_matrix: bfloat16 [64, 256, 1024], P('blk'), may hold values from -0.5 to 0.5
- middle_dense_matrix: bfloat16 [64, 1024, 1024], P('blk'), may hold values from -0.25 to 0.25
- closing_dense_matrix: bfloat16 [64, 1024, 1024], P('blk'), may hold values from -0.25 to 0.25
- final_readout_matrix: bfloat16 [64, 1024, 256], P('blk'), may hold values from -0.25 to 0.25
Outputs:
- new_east: bfloat16 [2048, 64, 128], P('blk', 'grp')
- new_north: bfloat16 [2048, 64, 128], P('blk', 'grp')
- new_pressure: bfloat16 [2048, 64, 128], P('blk', 'grp')
- heating: bfloat16 [2048, 64, 128], P('blk', 'grp')
- moistening: bfloat16 [2048, 64, 128], P('blk', 'grp')
Inputs may be any that keep to these rules, and one draw needn't show every extreme that they name: Each tile block, rows 32 * b to 32 * b + 31 of flow_category_label, holds exactly 32 columns of every regime.
All inputs are finite; a program needn't handle non-finite values.
Results may differ from a plain program's by a relative error of at most 0.012.
Values may be sent and summed in bfloat16 or wider, within the bound.
A program may use at most 64 MiB of HBM per device.

v0:
```python
import jax
import jax.numpy as jnp
from jax import lax
from jax.sharding import PartitionSpec as P

HEIGHT_COUNT = 128
SUB = 4


def with_halo(cells, sides, width):
    for axis, dim in sides:
        count = lax.axis_size(axis)
        head = lax.slice_in_dim(cells, 0, width, axis=dim)
        tail = lax.slice_in_dim(cells, cells.shape[dim] - width, cells.shape[dim], axis=dim)
        cells = jnp.concatenate(
            [
                lax.ppermute(tail, axis, [(i, (i + 1) % count) for i in range(count)]),
                cells,
                lax.ppermute(head, axis, [((i + 1) % count, i) for i in range(count)]),
            ],
            axis=dim,
        )
    return cells


def split_up(value, dim, peers):
    lengths = value.shape
    tiles = value.reshape(*lengths[:dim], peers, lengths[dim] // peers, *lengths[dim + 1 :])
    return jnp.moveaxis(tiles, dim, 0)


def sent_and_summed(value, axis, dim):
    peers = lax.axis_size(axis)
    tiles = lax.all_to_all(split_up(value, dim, peers), axis, 0, 0, tiled=True)
    return jnp.sum(tiles.astype(jnp.float32), axis=0)


def in_one_piece(arrays, axis, dim, along):
    widths = [a.shape[along] for a in arrays]
    both = jnp.concatenate(arrays, axis=along)
    out = sent_and_summed(both, axis, dim)
    return tuple(jnp.split(out, [sum(widths[:k]) for k in range(1, len(widths))], axis=along))


def cycle_diff(field):
    return (field[2:] - field[:-2]) * 0.5


def across_belt(field):
    padded = jnp.pad(field, ((0, 0), (1, 1), (0, 0)))
    return (padded[:, 2:] - padded[:, :-2]) * 0.5


def wind_update(eastward, northward, pressure_state, courant_rate):
    inner = pressure_state[1:-1]
    return (
        eastward[1:-1] - courant_rate * cycle_diff(pressure_state),
        northward[1:-1] - courant_rate * across_belt(inner),
        inner,
    )


def pressure_update(eastward, northward, pressure_state, courant_rate):
    inner_north = northward[1:-1]
    return (
        eastward[1:-1],
        inner_north,
        pressure_state[1:-1] - courant_rate * (cycle_diff(eastward) + across_belt(inner_north)),
    )


def network(columns, first, second, third, last):
    hidden = jax.nn.silu(jnp.dot(columns, first, preferred_element_type=jnp.float32)).astype(
        jnp.bfloat16
    )
    hidden = jax.nn.silu(jnp.dot(hidden, second, preferred_element_type=jnp.float32)).astype(
        jnp.bfloat16
    )
    hidden = jax.nn.silu(jnp.dot(hidden, third, preferred_element_type=jnp.float32)).astype(
        jnp.bfloat16
    )
    return jnp.dot(hidden, last, preferred_element_type=jnp.float32).astype(jnp.bfloat16)


def local(
    zonal_velocity_field,
    meridional_velocity_field,
    barometric_disturbance,
    delayed_thermal_deviation,
    delayed_moisture_deviation,
    flow_category_label,
    advective_stability_number,
    initial_dense_matrix,
    middle_dense_matrix,
    closing_dense_matrix,
    final_readout_matrix,
):
    group_index = lax.axis_index("grp")
    column_profile_width = 2 * HEIGHT_COUNT
    blocks = lax.axis_size("blk")
    atmosphere_soundings = jnp.concatenate(
        [delayed_thermal_deviation, delayed_moisture_deviation], axis=-1
    ).reshape(-1, column_profile_width)
    share = atmosphere_soundings.shape[0] // blocks
    sorting = jnp.argsort(flow_category_label.reshape(-1), stable=True)
    outgoing = jnp.take(atmosphere_soundings, sorting, axis=0).reshape(
        blocks, share, column_profile_width
    )
    half_width = zonal_velocity_field.shape[1] // 2
    pair_size = lax.axis_size("grp")
    part_rows = share // pair_size
    chosen = lax.dynamic_slice_in_dim(outgoing, group_index * part_rows, part_rows, 1)
    chosen_places = lax.dynamic_slice_in_dim(
        sorting.reshape(blocks, share), group_index * part_rows, part_rows, 1
    )
    arrived = lax.all_to_all(chosen, "blk", split_axis=0, concat_axis=0, tiled=True)
    columns = arrived.reshape(-1, column_profile_width)
    result = network(
        columns,
        initial_dense_matrix[0],
        middle_dense_matrix[0],
        closing_dense_matrix[0],
        final_readout_matrix[0],
    ).reshape(arrived.shape)
    returned = lax.all_to_all(result, "blk", split_axis=0, concat_axis=0, tiled=True)
    restored = (
        jnp.zeros((atmosphere_soundings.shape[0], column_profile_width), jnp.float32)
        .at[chosen_places.reshape(-1)]
        .set(returned.reshape(-1, column_profile_width).astype(jnp.float32))
    )
    tendency = restored.reshape(
        zonal_velocity_field.shape[0], zonal_velocity_field.shape[1], column_profile_width
    )
    heat_half, moist_half = in_one_piece(
        (
            tendency[:, :, :HEIGHT_COUNT].astype(jnp.bfloat16),
            tendency[:, :, HEIGHT_COUNT:].astype(jnp.bfloat16),
        ),
        "grp",
        1,
        0,
    )
    stacked = jnp.stack(
        [zonal_velocity_field, meridional_velocity_field, barometric_disturbance], axis=1
    )
    widened = with_halo(stacked, (("blk", 0),), 2 * SUB).astype(jnp.float32)
    eastward = widened[:, 0]
    northward = widened[:, 1]
    pressure_state = widened[:, 2]
    for substep in range(SUB):
        eastward, northward, pressure_state = wind_update(
            eastward, northward, pressure_state, advective_stability_number
        )
        eastward, northward, pressure_state = pressure_update(
            eastward, northward, pressure_state, advective_stability_number
        )
    dynamic_fields = (
        eastward.astype(jnp.bfloat16),
        northward.astype(jnp.bfloat16),
        pressure_state.astype(jnp.bfloat16),
    )
    own_start = group_index * half_width
    owned = [lax.dynamic_slice_in_dim(field, own_start, half_width, 1) for field in dynamic_fields]
    return (
        owned[0],
        owned[1],
        owned[2],
        heat_half.astype(jnp.bfloat16),
        moist_half.astype(jnp.bfloat16),
    )


def solution(mesh):
    return jax.shard_map(
        local,
        mesh=mesh,
        in_specs=(
            P("blk", None, None),
            P("blk", None, None),
            P("blk", None, None),
            P("blk", None, None),
            P("blk", None, None),
            P("blk", None),
            P(),
            P("blk", None, None),
            P("blk", None, None),
            P("blk", None, None),
            P("blk", None, None),
        ),
        out_specs=(
            P("blk", "grp", None),
            P("blk", "grp", None),
            P("blk", "grp", None),
            P("blk", "grp", None),
            P("blk", "grp", None),
        ),
        check_vma=False,
    )
```

profile of v0, /device:TPU:1, one launch (start us, length us, event | category | flops | bytes accessed | tf_op | source)
XLA Modules:
  0.0 117.6 jit_solution(13206215831236438403)
XLA Ops:
  0.7 2.3 %pad_maximum_fusion.4 = (bf16[8,3,64,128]{3,2,0,1:T(8,128)(2,1)}, bf16[8,3,64,128]{3,2,0,1:T(8,128)(2,1)}) fusion(bf16[32,1,64,128]{3,2,0,1:T(8,128)(2,1)} %bitcast.56, bf16[32,1,64,128]{3,2,0,1:T(8,128)(2,1)} %bitcast.58, bf16[32,1,64,128]{3,2,0,1:T(8,128)(2,1)} %bitcast.60), kind=kLoop, calls=%fused_computation.91 | loop fusion | flops 786432 | bytes 2359296 | tf_op jit(solution)/shard_map/slice | solution.py:14
  3.0 3.0 %collective-permute-start = (bf16[8,3,64,128]{3,2,0,1:T(8,128)(2,1)}, bf16[8,3,64,128]{3,2,0,1:T(8,128)(2,1)S(1)}, u32[]{:S(2)}, u32[]{:S(2)}) collective-permute-start(bf16[8,3,64,128]{3,2,0,1:T(8,128)(2,1)} %get-tuple-element.9), channel_id=1, source_target_pairs={{0,1},{1,2},{2,3},{3,4},{4,5},{5,6},{6,7},{7,8},{8,9},{9,10},{10,1... | collective-permute-start | bytes 1179656 | tf_op jit(solution)/shard_map/ppermute | solution.py:17
  6.1 5.0 %sort.17 = (s32[2048]{0:T(1024)}, s32[2048]{0:T(1024)S(1)}) sort(s32[2048]{0:T(1024)S(1)} %reshape.85, s32[2048]{0:T(1024)S(1)} %iota.4), dimensions={0}, to_apply=%region_0.0 | sort | flops 22528 | bytes 32768 | tf_op jit(solution)/shard_map/jit(argsort)/sort | solution.py:105
  11.9 1.3 %pad_maximum_fusion = bf16[32,64,256]{2,1,0:T(8,128)(2,1)S(1)} fusion(bf16[32,64,128]{2,1,0:T(8,128)(2,1)} %param.15, bf16[32,64,128]{2,1,0:T(8,128)(2,1)} %param.14), kind=kLoop, calls=%fused_computation.73 | loop fusion | flops 2097152 | bytes 2097152 | tf_op jit(solution)/shard_map/concatenate | solution.py:101
  13.2 9.8 %gather_fusion = bf16[2048,256]{1,0:T(8,128)(2,1)} fusion(bf16[2048,256]{1,0:T(8,128)(2,1)S(1)} %bitcast.52, s32[2048]{0:T(1024)} %fusion.52), kind=kCustom, calls=%fused_computation | custom fusion | bytes 2105344 | tf_op jit(solution)/shard_map/jit(_take)/gather | solution.py:106
  23.0 2.2 %dynamic-slice_select_fusion = bf16[64,16,256]{2,1,0:T(8,128)(2,1)} fusion(bf16[64,32,256]{2,1,0:T(8,128)(2,1)} %bitcast.55, s32[]{:T(128)S(6)} %select_n.30, pred[64,16]{1,0:T(8,128)(4,1)S(1)} %constant_dynamic-slice_fusion), kind=kLoop, calls=%fused_computation.78 | loop fusion | flops 262144 | bytes 1049604 | tf_op jit(solution)/shard_map/jit(_take)/select_n | solution.py:106
  25.2 11.7 %all-to-all-start = ((bf16[64,16,256]{2,1,0:T(8,128)(2,1)}), bf16[64,16,256]{2,1,0:T(8,128)(2,1)}, u32[]{:S(2)}, u32[]{:S(2)}) async-start(bf16[64,16,256]{2,1,0:T(8,128)(2,1)} %dynamic-slice_select_fusion), calls=%async_computation | async-start | bytes 1048576 | tf_op jit(solution)/shard_map/all_to_all | solution.py:116
  37.6 1.4 %constant_dynamic-slice_fusion.1 = s32[64,16]{1,0:T(8,128)} fusion(s32[64,32]{1,0:T(8,128)} %reshape.86, s32[]{:T(128)S(6)} %select_n.30), kind=kLoop, calls=%fused_computation.97 | loop fusion | bytes 8196 | tf_op jit(solution)/shard_map/dynamic_slice | solution.py:113
  40.6 1.6 %maximum_convert_fusion = f32[48,3,64,128]{3,2,0,1:T(8,128)S(1)} fusion(bf16[8,3,64,128]{3,2,0,1:T(8,128)(2,1)} %collective-permute-done.1, bf16[32,1,64,128]{3,2,0,1:T(8,128)(2,1)S(1)} %bitcast.57, bf16[32,1,64,128]{3,2,0,1:T(8,128)(2,1)S(1)} %bitcast.59, bf16[32,1,64,128]{3,2,0,1:T(8,128)(2,1)} %bitcast.61, bf16[8,3,64,128]{3,2,0,1:T(8,128)(2,1)S(1)} %collective-permute-done), kind=kLoop, calls=%fused_computation.5 | loop fusion | flops 5898240 | bytes 7077888 | tf_op jit(solution)/shard_map/convert_element_type | solution.py:146
  42.3 1.2 %fusion.12 = (f32[46,64,128]{2,1,0:T(8,128)S(1)}, f32[46,64,128]{2,1,0:T(8,128)S(1)}) fusion(f32[48,3,64,128]{3,2,0,1:T(8,128)S(1)} %maximum_convert_fusion, f32[128]{0:T(128)S(1)} %broadcast_multiply_fusion, f32[46,64,128]{2,1,0:T(8,128)S(1)} %slice_bitcast_fusion), kind=kLoop, calls=%fused_computation.26 | loop fusion | flops 2260992 | bytes 10551808 | tf_op jit(solution)/shard_map/sub | solution.py:57
  47.4 1.7 %fusion.56 = (f32[34,64,128]{2,1,0:T(8,128)}, f32[34,64,128]{2,1,0:T(8,128)}) fusion(f32[36,64,128]{2,1,0:T(8,128)S(1)} %fusion.35, f32[128]{0:T(128)S(1)} %broadcast_multiply_fusion, f32[38,64,128]{2,1,0:T(8,128)S(1)} %get-tuple-element.13), kind=kLoop, calls=%fused_computation.101 | loop fusion | flops 835584 | bytes 6685184 | tf_op jit(solution)/shard_map/slice | solution.py:55
  49.1 1.7 %all-to-all-done = bf16[64,16,256]{2,1,0:T(8,128)(2,1)} async-done(((bf16[64,16,256]{2,1,0:T(8,128)(2,1)}), bf16[64,16,256]{2,1,0:T(8,128)(2,1)}, u32[]{:S(2)}, u32[]{:S(2)}) %all-to-all-start) | async-done | bytes 524320 | tf_op jit(solution)/shard_map/all_to_all | solution.py:116
  50.9 6.4 %fusion.2 = f32[1024,1024]{1,0:T(8,128)} fusion(bf16[1,1024,1024]{2,1,0:T(8,128)(2,1)S(1)} %copy-done, bf16[1024,256]{1,0:T(8,128)(2,1)} %bitcast.11, bf16[1,256,1024]{2,1,0:T(8,128)(2,1)} %param.18), kind=kOutput, calls=%fused_computation.8 | convolution fusion | flops 2689597440 | bytes 7340032 | tf_op jit(solution)/shard_map/dot_general | solution.py:76
  57.3 7.4 %fusion.26 = bf16[1024,256]{1,0:T(8,128)(2,1)} fusion(bf16[1,1024,1024]{2,1,0:T(8,128)(2,1)} %param.20, f32[1024,1024]{1,0:T(8,128)} %fusion.2, bf16[1,1024,256]{2,1,0:T(8,128)(2,1)} %param.21), kind=kOutput, calls=%fused_computation.51 | convolution fusion | flops 2695102464 | bytes 7340032 | tf_op jit(solution)/shard_map/dot_general | solution.py:82
  64.7 9.0 %all-to-all-start.1 = ((bf16[64,16,256]{2,1,0:T(8,128)(2,1)}), bf16[64,16,256]{2,1,0:T(8,128)(2,1)}, u32[]{:S(2)}, u32[]{:S(2)}) async-start(bf16[64,16,256]{2,1,0:T(8,128)(2,1)} %bitcast.62), calls=%async_computation.1 | async-start | bytes 1048576 | tf_op jit(solution)/shard_map/all_to_all | solution.py:125
  73.6 2.1 %pad_slice_fusion.13 = (f32[34,64,128]{2,1,0:T(8,128)S(1)}, f32[34,64,128]{2,1,0:T(8,128)S(1)}) fusion(f32[34,64,128]{2,1,0:T(8,128)} %get-tuple-element.15), kind=kLoop, calls=%fused_computation.53 | loop fusion | bytes 3342336 | tf_op jit(solution)/shard_map/slice | solution.py:51
  75.7 1.4 %slice.302 = bf16[32,64,128]{2,1,0:T(8,128)(2,1)S(1)} slice(f32[34,64,128]{2,1,0:T(8,128)} %get-tuple-element.16), slice={[1:33], [0:64], [0:128]} | slice | bytes 1048576 | tf_op jit(solution)/shard_map/slice | solution.py:66
  79.5 8.0 %all-to-all-done.1 = bf16[64,16,256]{2,1,0:T(8,128)(2,1)} async-done(((bf16[64,16,256]{2,1,0:T(8,128)(2,1)}), bf16[64,16,256]{2,1,0:T(8,128)(2,1)}, u32[]{:S(2)}, u32[]{:S(2)}) %all-to-all-start.1) | async-done | bytes 524320 | tf_op jit(solution)/shard_map/all_to_all | solution.py:125
  87.4 6.7 %scatter_custom_fusion = f32[2048,256]{1,0:T(8,128)} fusion(s32[1024]{0:T(1024)S(1)} %bitcast.63, bf16[1024,256]{1,0:T(8,128)(2,1)} %bitcast.21, f32[]{:T(128)} %constant.13.clone.1), kind=kCustom, calls=%fused_computation.75 | custom fusion | flops 262144 | bytes 2621444 | tf_op jit(solution)/shard_map/scatter | solution.py:129
  94.1 1.7 %convert.16 = bf16[2048,256]{1,0:T(8,128)(2,1)S(1)} convert(f32[2048,256]{1,0:T(8,128)} %scatter_custom_fusion) | non-fusion elementwise | flops 524288 | bytes 3145728 | tf_op jit(solution)/shard_map/convert.4
  97.3 4.5 %all-to-all-start.2 = ((bf16[2,64,32,128]{3,2,1,0:T(8,128)(2,1)}), bf16[2,64,32,128]{3,2,1,0:T(8,128)(2,1)}, u32[]{:S(2)}, u32[]{:S(2)}) async-start(bf16[2,64,32,128]{3,2,1,0:T(8,128)(2,1)} %copy.16), calls=%async_computation.2 | async-start | bytes 2097152 | tf_op jit(solution)/shard_map/all_to_all | solution.py:34
  101.9 2.3 %pad_slice_fusion.15 = (f32[32,64,128]{2,1,0:T(8,128)S(1)}, f32[32,64,128]{2,1,0:T(8,128)S(1)}, f32[32,64,128]{2,1,0:T(8,128)S(1)}, f32[32,64,128]{2,1,0:T(8,128)S(1)}) fusion(f32[32,64,128]{2,1,0:T(8,128)} %copy-done.4, f32[34,64,128]{2,1,0:T(8,128)S(1)} %copy-done.2), kind=kLoop, calls=%fused_computation.66 | loop fusion | bytes 7340032 | tf_op jit(solution)/shard_map/slice | solution.py:51
  105.2 10.0 %all-to-all-done.2 = bf16[2,64,32,128]{3,2,1,0:T(8,128)(2,1)} async-done(((bf16[2,64,32,128]{3,2,1,0:T(8,128)(2,1)}), bf16[2,64,32,128]{3,2,1,0:T(8,128)(2,1)}, u32[]{:S(2)}, u32[]{:S(2)}) %all-to-all-start.2) | async-done | bytes 1048608 | tf_op jit(solution)/shard_map/all_to_all | solution.py:34
  115.1 1.7 %reduce = bf16[64,32,128]{2,1,0:T(8,128)(2,1)S(1)} reduce(bf16[2,64,32,128]{3,2,1,0:T(8,128)(2,1)} %all-to-all-done.2, bf16[]{:T(256)} %constant.75), dimensions={0}, to_apply=%region_2.3.clone | reduce | flops 262144 | bytes 1572866 | tf_op jit(solution)/shard_map/reduce_sum | solution.py:35
  (51 shorter events, 12.6 us)
Async XLA Ops:
  0.6 50.2 %copy-start = (bf16[1,1024,1024]{2,1,0:T(8,128)(2,1)S(1)}, bf16[1,1024,1024]{2,1,0:T(8,128)(2,1)}, u32[]{:S(2)}) copy-start(bf16[1,1024,1024]{2,1,0:T(8,128)(2,1)} %param.19) | copy-start | bytes 6291460
  0.6 5.4 %copy-start.7 = (s32[32,64]{1,0:T(8,128)S(1)}, s32[32,64]{1,0:T(8,128)}, u32[]{:S(2)}) copy-start(s32[32,64]{1,0:T(8,128)} %param.16) | copy-start | bytes 24580
  3.0 37.6 %collective-permute-start = (bf16[8,3,64,128]{3,2,0,1:T(8,128)(2,1)}, bf16[8,3,64,128]{3,2,0,1:T(8,128)(2,1)S(1)}, u32[]{:S(2)}, u32[]{:S(2)}) collective-permute-start(bf16[8,3,64,128]{3,2,0,1:T(8,128)(2,1)} %get-tuple-element.9), channel_id=1, source_target_pairs={{0,1},{1,2},{2,3},{3,4},{4,5},{5,6},{6,7},{7,8},{8,9},{9,10},{10,1... | collective-permute-start | bytes 1179656 | tf_op jit(solution)/shard_map/ppermute | solution.py:17
  6.0 34.6 %collective-permute-start.1 = (bf16[8,3,64,128]{3,2,0,1:T(8,128)(2,1)}, bf16[8,3,64,128]{3,2,0,1:T(8,128)(2,1)}, u32[]{:S(2)}, u32[]{:S(2)}) collective-permute-start(bf16[8,3,64,128]{3,2,0,1:T(8,128)(2,1)} %get-tuple-element.10), channel_id=1, source_target_pairs={{1,0},{2,1},{3,2},{4,3},{5,4},{6,5},{7,6},{8,7},{9,8},{10,9},{11,1... | collective-permute-start | bytes 1179656 | tf_op jit(solution)/shard_map/ppermute | solution.py:19
  23.0 17.6 %copy-start.5 = (bf16[32,64,128]{2,1,0:T(8,128)(2,1)S(1)}, bf16[32,64,128]{2,1,0:T(8,128)(2,1)}, u32[]{:S(2)}) copy-start(bf16[32,64,128]{2,1,0:T(8,128)(2,1)} %param.13) | copy-start | bytes 1572868
  23.0 17.6 %copy-start.6 = (bf16[32,64,128]{2,1,0:T(8,128)(2,1)S(1)}, bf16[32,64,128]{2,1,0:T(8,128)(2,1)}, u32[]{:S(2)}) copy-start(bf16[32,64,128]{2,1,0:T(8,128)(2,1)} %param.12) | copy-start | bytes 1572868
  25.2 25.7 %all-to-all-start = ((bf16[64,16,256]{2,1,0:T(8,128)(2,1)}), bf16[64,16,256]{2,1,0:T(8,128)(2,1)}, u32[]{:S(2)}, u32[]{:S(2)}) async-start(bf16[64,16,256]{2,1,0:T(8,128)(2,1)} %dynamic-slice_select_fusion), calls=%async_computation | async-start | bytes 1048576 | tf_op jit(solution)/shard_map/all_to_all | solution.py:116
  46.3 1.1 copy-start.3
  47.4 28.3 %copy-start.1 = (f32[36,64,128]{2,1,0:T(8,128)}, f32[36,64,128]{2,1,0:T(8,128)S(1)}, u32[]{:S(2)}) copy-start(f32[36,64,128]{2,1,0:T(8,128)S(1)} %fusion.35) | copy-start | bytes 3538948
  64.7 22.8 %all-to-all-start.1 = ((bf16[64,16,256]{2,1,0:T(8,128)(2,1)}), bf16[64,16,256]{2,1,0:T(8,128)(2,1)}, u32[]{:S(2)}, u32[]{:S(2)}) async-start(bf16[64,16,256]{2,1,0:T(8,128)(2,1)} %bitcast.62), calls=%async_computation.1 | async-start | bytes 1048576 | tf_op jit(solution)/shard_map/all_to_all | solution.py:125
  75.7 1.6 %slice-start.1 = ((f32[38,64,128]{2,1,0:T(8,128)}), f32[34,64,128]{2,1,0:T(8,128)S(1)}, s32[]{:S(2)}) async-start(f32[38,64,128]{2,1,0:T(8,128)} %copy-done.3), calls=%async_computation.4 | async-start | bytes 2228224 | tf_op jit(solution)/shard_map/slice | solution.py:58
  77.7 1.0 copy-start.4
  97.3 4.5 %copy-start.2 = (f32[34,64,128]{2,1,0:T(8,128)S(1)}, f32[34,64,128]{2,1,0:T(8,128)}, u32[]{:S(2)}) copy-start(f32[34,64,128]{2,1,0:T(8,128)} %get-tuple-element.16) | copy-start | bytes 3342340
  97.3 17.8 %all-to-all-start.2 = ((bf16[2,64,32,128]{3,2,1,0:T(8,128)(2,1)}), bf16[2,64,32,128]{3,2,1,0:T(8,128)(2,1)}, u32[]{:S(2)}, u32[]{:S(2)}) async-start(bf16[2,64,32,128]{3,2,1,0:T(8,128)(2,1)} %copy.16), calls=%async_computation.2 | async-start | bytes 2097152 | tf_op jit(solution)/shard_map/all_to_all | solution.py:34
  101.8 2.3 %slice-start = ((f32[36,64,128]{2,1,0:T(8,128)}), f32[32,64,128]{2,1,0:T(8,128)S(1)}, s32[]{:S(2)}) async-start(f32[36,64,128]{2,1,0:T(8,128)} %copy-done.1), calls=%async_computation.3 | async-start | bytes 2097152 | tf_op jit(solution)/shard_map/slice | solution.py:68
where the time goes:
time: 119 us; the launch traced here: 118 us
  other arithmetic  31.2 us (26%)
  starting transfers between devices  28.2 us (24%)
  local copies, waits for them, and re-layouts  23.8 us (20%)
  waiting for transfers between devices  19.6 us (16%)
  matrix products  13.8 us (12%)
    all_to_all x1, starting transfers between devices, local(): lax.all_to_all(chosen, 'blk', split_axis=0, concat_axis=0, tiled=True)  11.7 us
    all_to_all x1, waiting for transfers between devices, sent_and_summed(): tiles = lax.all_to_all(split_up(value, dim, peers), axis, 0, 0, tiled=True)  9.96 us
    gather x1, local copies, waits for them, and re-layouts, local(): jnp.take(atmosphere_soundings, sorting, axis=0)  9.76 us
    all_to_all x1, starting transfers between devices, local(): lax.all_to_all(result, 'blk', split_axis=0, concat_axis=0, tiled=True)  8.95 us
    all_to_all x1, waiting for transfers between devices, local(): lax.all_to_all(result, 'blk', split_axis=0, concat_axis=0, tiled=True)  7.97 us
    dot_general x1, matrix products, network(): jnp.dot(hidden, last, preferred_element_type=jnp.float32)  7.36 us
    scatter x1, other arithmetic, local(): restored = jnp.zeros((atmosphere_soundings.shape[0], column_profile_width...  6.68 us
    dot_general x1, matrix products, network(): jnp.dot(hidden, second, preferred_element_type=jnp.float32)  6.43 us
  transfers between devices with their start and end apart: 5, of which 3 were waited for; matrix products, arithmetic and copies ran while one was open for 33% of the time, Pallas kernels for 0%

commit v1 on v0

v1 whole, which is shorter than its diff:
```python
import functools

import jax
import jax.numpy as jnp
from jax import lax
from jax.experimental import pallas as pl
from jax.experimental.pallas import tpu as pltpu
from jax.sharding import PartitionSpec as P

MESH = pl.DeviceIdType.MESH
SUB = 4
HALO = 2 * SUB
CX, HALF, LEV = 32, 32, 128
COLS = 2 * CX * HALF
WJ = HALF + HALO
ROWS = CX + 2 * HALO
PEERS, PIECE = 64, 16
MINE = PEERS * PIECE
CHUNKS = 4
PER = PEERS // CHUNKS
CROWS = PER * PIECE
BF, F32 = jnp.bfloat16, jnp.float32


def silu(s):
    half = s * 0.5
    return half * jnp.tanh(half) + half


def offset(o):
    dy = (o // 4) % 4
    return dy, (o // 2) % 2, (o // 16 - dy + 4) % 4, o % 2


def peer(o, sign, g, b):
    dy, dx, dz, dc = offset(o)
    y = (b // 16 + sign * dy + 4) % 4
    x = (b // 8 + dx) % 2
    z = ((b // 2) % 4 + sign * dz + 4) % 4
    c = (b + dc) % 2
    return {"grp": (g + dx) % 2, "blk": ((y * 2 + x) * 4 + z) * 2 + c}


def slots_of(lab, ot, cum, rank, g, b):
    labels = lab[...]
    sub = lax.broadcasted_iota(jnp.int32, (64, 128), 0)
    for k in range(16):
        hit = jnp.where(labels[k : k + 1, :] == sub, 1.0, 0.0)
        ot[k * 64 : (k + 1) * 64, :] = hit.astype(BF)
    row = lax.broadcasted_iota(jnp.int32, (128, 256), 0)
    col = lax.broadcasted_iota(jnp.int32, (128, 256), 1)
    tri = jnp.where((row < col) | (col >= 128), 1.0, 0.0).astype(BF)
    cum[...] = jnp.dot(ot[...], tri, preferred_element_type=F32)
    base = jnp.zeros((64, 128), F32)
    for k in range(16):
        hit = ot[k * 64 : (k + 1) * 64, :].astype(F32)
        before = cum[k * 64 : (k + 1) * 64, :128] + base
        rank[k : k + 1, :] = jnp.sum(hit * before, axis=0, keepdims=True)
        base = base + cum[k * 64 : (k + 1) * 64, 128:]
    place = rank[...].astype(jnp.int32)
    dy = ((labels >> 4) - b // 16 + 4) & 3
    dx = ((labels >> 3) + b // 8) & 1
    dz = ((labels >> 1) - (b // 2) % 4 + 4) & 3
    dc = (labels + b) & 1
    o = ((dy + dz) & 3) * 16 + dy * 4 + dx * 2 + dc
    side = ((place >> 4) + g + dx) & 1
    return side * MINE + o * PIECE + (place & (PIECE - 1))


def slope(x):
    edge = lax.broadcasted_iota(jnp.int32, x.shape, 0)
    up = jnp.where(edge == x.shape[0] - 1, 0.0, pltpu.roll(x, x.shape[0] - 1, 0))
    down = jnp.where(edge == 0, 0.0, pltpu.roll(x, 1, 0))
    return up - down


def substep(s, rate, east, north, press):
    lo, hi = 2 * (s + 1), ROWS - 2 * (s + 1)
    half = jnp.broadcast_to(rate[...] * 0.5, (WJ, LEV))
    p_lo, p_next = press[lo], press[lo + 1]
    e_before = east[lo - 1] - half * (p_lo - press[lo - 2])
    e_here = east[lo] - half * (p_next - press[lo - 1])
    east[lo - 1] = e_before
    east[lo] = e_here

    def step(i, carry):
        e_before, e_here, p_here, p_next = carry
        p_after = press[i + 2]
        e_next = east[i + 1] - half * (p_after - p_here)
        east[i + 1] = e_next
        n_here = north[i] - half * slope(p_here)
        north[i] = n_here
        press[i] = p_here - half * ((e_next - e_before) + slope(n_here))
        return e_here, e_next, p_next, p_after

    lax.fori_loop(lo, hi, step, (e_before, e_here, p_lo, p_next))


def main_kernel(
    lab, rate, therm, moist, zonal, merid, baro, w1h, w2h, w3h, w4h,
    back, slots, east_o, north_o, press_o,
    prof, pbuf, ot, cum, rank, send, recv, res, hid_a, hid_b, mine, theirs,
    w1, w2, w3, w4, stage, east, north, press,
    load_sem, weight_sem, out_sem, fs_sem, fr_sem, rs_sem, rr_sem, ps_sem, pr_sem, hs_sem, hr_sem,
):
    g = lax.axis_index("grp")
    b = lax.axis_index("blk")
    partner = {"grp": (g + 1) % 2, "blk": b}
    right = {"grp": g, "blk": (b + 1) % 64}
    left = {"grp": g, "blk": (b + 63) % 64}

    loads = []
    for h in range(2):
        for f, src in enumerate((therm, moist)):
            loads.append(
                pltpu.make_async_copy(
                    src.at[:, pl.ds(h * HALF, HALF), :],
                    prof.at[h, :, :, pl.ds(f * LEV, LEV)],
                    load_sem.at[2 * h + f],
                )
            )
    fields = []
    window = pl.multiple_of(g * (HALF - HALO), 8)
    for f, src in enumerate((zonal, merid, baro)):
        fields.append(
            pltpu.make_async_copy(
                src.at[:, pl.ds(window, WJ), :],
                stage.at[f, pl.ds(HALO, CX)],
                load_sem.at[4 + f],
            )
        )
    weights = [
        pltpu.make_async_copy(src.at[0], dst, weight_sem.at[n])
        for n, (src, dst) in enumerate(((w1h, w1), (w2h, w2), (w3h, w3), (w4h, w4)))
    ]
    for copy in loads + fields + weights:
        copy.start()

    barrier = pltpu.get_barrier_semaphore()

    def greet(o, carry):
        pl.semaphore_signal(barrier, inc=1, device_id=peer(o, 1, g, b), device_id_type=MESH)
        return carry

    lax.fori_loop(1, PEERS, greet, 0)
    for other in (partner, left, right):
        pl.semaphore_signal(barrier, inc=1, device_id=other, device_id_type=MESH)

    slot = slots_of(lab, ot, cum, rank, g, b)
    slots[...] = slot
    for copy in loads:
        copy.wait()

    def gather(m, carry):
        want = lax.broadcasted_iota(jnp.int32, (CROWS, 128), 0) + m * CROWS
        for k in range(16):
            hit = jnp.where(slots[k : k + 1, :] == want, 1.0, 0.0)
            pbuf[:, k * 128 : (k + 1) * 128] = hit.astype(BF)
        rows = jnp.dot(pbuf[...], prof[...].reshape(COLS, 2 * LEV), preferred_element_type=F32)
        send[pl.ds(pl.multiple_of(m * CROWS, CROWS), CROWS), :] = rows.astype(BF)
        return carry

    lax.fori_loop(0, CHUNKS, gather, 0)
    recv[0:PIECE, :] = send[0:PIECE, :]
    pl.semaphore_wait(barrier, PEERS - 1 + 3)

    def piece(o):
        return pl.ds(pl.multiple_of(o * PIECE, PIECE), PIECE)

    def forth(o):
        return pltpu.make_async_remote_copy(
            src_ref=send.at[piece(o)],
            dst_ref=recv.at[piece(o)],
            send_sem=fs_sem.at[o],
            recv_sem=fr_sem.at[o],
            device_id=peer(o, 1, g, b),
            device_id_type=MESH,
        )

    def home(o):
        return pltpu.make_async_remote_copy(
            src_ref=res.at[piece(o)],
            dst_ref=mine.at[piece(o)],
            send_sem=rs_sem.at[o],
            recv_sem=rr_sem.at[o],
            device_id=peer(o, -1, g, b),
            device_id_type=MESH,
        )

    def across(k):
        rows = pl.ds(pl.multiple_of(k * CROWS, CROWS), CROWS)
        return pltpu.make_async_remote_copy(
            src_ref=mine.at[rows],
            dst_ref=theirs.at[rows],
            send_sem=ps_sem.at[k],
            recv_sem=pr_sem.at[k],
            device_id=partner,
            device_id_type=MESH,
        )

    def each(first, last, act):
        def body(o, carry):
            act(o)
            return carry

        lax.fori_loop(first, last, body, 0)

    each(1, PEERS, lambda o: forth(o).start())
    for copy in fields:
        copy.wait()
    halos = [
        pltpu.make_async_remote_copy(
            src_ref=stage.at[:, pl.ds(src, HALO)],
            dst_ref=stage.at[:, pl.ds(dst, HALO)],
            send_sem=hs_sem.at[n],
            recv_sem=hr_sem.at[n],
            device_id=other,
            device_id_type=MESH,
        )
        for n, (src, dst, other) in enumerate(((CX, 0, right), (HALO, HALO + CX, left)))
    ]
    for copy in halos:
        copy.start()
    for copy in weights:
        copy.wait()

    def hand_on(k):
        each(jnp.maximum(k * PER, 1), (k + 1) * PER, lambda o: home(o).wait_recv())
        across(k).start()

    def network(k):
        rows = pl.ds(pl.multiple_of(k * CROWS, CROWS), CROWS)
        x = recv[rows, :]
        for n in range(4):
            cut = slice(n * 256, (n + 1) * 256)
            hid_a[:, cut] = silu(jnp.dot(x, w1[:, cut], preferred_element_type=F32)).astype(BF)
        for n in range(4):
            cut = slice(n * 256, (n + 1) * 256)
            hid_b[:, cut] = silu(jnp.dot(hid_a[...], w2[:, cut], preferred_element_type=F32)).astype(BF)
        for n in range(4):
            cut = slice(n * 256, (n + 1) * 256)
            hid_a[:, cut] = silu(jnp.dot(hid_b[...], w3[:, cut], preferred_element_type=F32)).astype(BF)
        res[rows, :] = jnp.dot(hid_a[...], w4[...], preferred_element_type=F32).astype(BF)

    def turn(k, carry):
        each(jnp.maximum(k * PER, 1), (k + 1) * PER, lambda o: forth(o).wait_recv())
        network(k)
        each(jnp.maximum(k * PER, 1), (k + 1) * PER, lambda o: home(o).start())

        @pl.when(k == 0)
        def _():
            mine[0:PIECE, :] = res[0:PIECE, :]

        @pl.when(k >= 1)
        def _():
            hand_on(k - 1)

        return carry

    lax.fori_loop(0, CHUNKS, turn, 0)

    for copy in halos:
        copy.wait()

    def widen(i, carry):
        east[i] = stage[0, i].astype(F32)
        north[i] = stage[1, i].astype(F32)
        press[i] = stage[2, i].astype(F32)
        return carry

    lax.fori_loop(0, ROWS, widen, 0)
    substep(0, rate, east, north, press)
    hand_on(CHUNKS - 1)
    for s in range(1, SUB):
        substep(s, rate, east, north, press)
    own = pl.ds(pl.multiple_of(g * HALO, 8), HALF)

    def narrow(i, carry):
        east_o[i] = east[i + HALO, own].astype(BF)
        north_o[i] = north[i + HALO, own].astype(BF)
        press_o[i] = press[i + HALO, own].astype(BF)
        return carry

    lax.fori_loop(0, CX, narrow, 0)

    each(0, CHUNKS, lambda k: across(k).wait_send())
    out_mine = pltpu.make_async_copy(mine, back.at[pl.ds(0, MINE)], out_sem.at[0])
    out_mine.start()
    each(0, CHUNKS, lambda k: across(k).wait_recv())
    out_theirs = pltpu.make_async_copy(theirs, back.at[pl.ds(MINE, MINE)], out_sem.at[1])
    out_theirs.start()
    each(1, PEERS, lambda o: forth(o).wait_send())
    each(1, PEERS, lambda o: home(o).wait_send())
    out_mine.wait()
    out_theirs.wait()


def place_kernel(slots, back, east, north, press, east_o, north_o, press_o, heat, moist):
    g = lax.axis_index("grp")
    own = slots[pl.ds(pl.multiple_of(g * 8, 8), 8), :].astype(F32)
    columns = jnp.transpose(own).astype(jnp.int32)
    lane = lax.broadcasted_iota(jnp.int32, (128, 2 * MINE), 1)
    for k in range(4):
        hits = [
            jnp.where(columns[:, 2 * k + q : 2 * k + q + 1] == lane, 1.0, 0.0).astype(BF)
            for q in range(2)
        ]
        rows = jnp.dot(jnp.concatenate(hits, axis=0), back[...], preferred_element_type=F32)
        heat[k * 256 : (k + 1) * 256, :] = rows[:, :LEV].astype(BF)
        moist[k * 256 : (k + 1) * 256, :] = rows[:, LEV:].astype(BF)
    east_o[...] = east[...]
    north_o[...] = north[...]
    press_o[...] = press[...]


def local(zonal, merid, baro, therm, moist, labels, rate, w1, w2, w3, w4):
    lab = labels.reshape(CX, 2, HALF).transpose(1, 0, 2).reshape(16, 128)
    vmem = pl.BlockSpec(memory_space=pltpu.VMEM)
    hbm = pl.BlockSpec(memory_space=pl.ANY)
    field = jax.ShapeDtypeStruct((CX, HALF, LEV), BF)
    dma = pltpu.SemaphoreType.DMA
    hid = w2.shape[-1]
    back, slots, east, north, press = pl.pallas_call(
        main_kernel,
        out_shape=(
            jax.ShapeDtypeStruct((2 * MINE, 2 * LEV), BF),
            jax.ShapeDtypeStruct((16, 128), jnp.int32),
            field, field, field,
        ),
        in_specs=[vmem, vmem] + [hbm] * 9,
        out_specs=(hbm, vmem, vmem, vmem, vmem),
        scratch_shapes=[
            pltpu.VMEM((2, CX, HALF, 2 * LEV), BF),
            pltpu.VMEM((CROWS, COLS), BF),
            pltpu.VMEM((1024, 128), BF),
            pltpu.VMEM((1024, 256), F32),
            pltpu.VMEM((16, 128), F32),
            pltpu.VMEM((MINE, 2 * LEV), BF),
            pltpu.VMEM((MINE, 2 * LEV), BF),
            pltpu.VMEM((MINE, 2 * LEV), BF),
            pltpu.VMEM((CROWS, hid), BF),
            pltpu.VMEM((CROWS, hid), BF),
            pltpu.VMEM((MINE, 2 * LEV), BF),
            pltpu.VMEM((MINE, 2 * LEV), BF),
            pltpu.VMEM(w1.shape[1:], BF),
            pltpu.VMEM(w2.shape[1:], BF),
            pltpu.VMEM(w3.shape[1:], BF),
            pltpu.VMEM(w4.shape[1:], BF),
            pltpu.VMEM((3, ROWS, WJ, LEV), BF),
            pltpu.VMEM((ROWS, WJ, LEV), F32),
            pltpu.VMEM((ROWS, WJ, LEV), F32),
            pltpu.VMEM((ROWS, WJ, LEV), F32),
            dma((7,)), dma((4,)), dma((2,)),
            dma((PEERS,)), dma((PEERS,)), dma((PEERS,)), dma((PEERS,)),
            dma((CHUNKS,)), dma((CHUNKS,)), dma((2,)), dma((2,)),
        ],
        compiler_params=pltpu.CompilerParams(
            collective_id=0, has_side_effects=True, vmem_limit_bytes=40 * 1024 * 1024
        ),
        name="main",
    )(lab, rate.reshape(1, LEV), therm, moist, zonal, merid, baro, w1, w2, w3, w4)
    flat = jax.ShapeDtypeStruct((CX * HALF, LEV), BF)
    east, north, press, heat, moistening = pl.pallas_call(
        place_kernel,
        out_shape=(field, field, field, flat, flat),
        in_specs=[vmem] * 5,
        out_specs=(vmem,) * 5,
        compiler_params=pltpu.CompilerParams(vmem_limit_bytes=32 * 1024 * 1024),
        name="place",
    )(slots, back, east, north, press)
    return east, north, press, heat.reshape(CX, HALF, LEV), moistening.reshape(CX, HALF, LEV)


def solution(mesh):
    whole = P("blk", None, None)
    out = P("blk", "grp", None)
    return jax.shard_map(
        local,
        mesh=mesh,
        in_specs=(whole,) * 5 + (P("blk", None), P()) + (whole,) * 4,
        out_specs=(out,) * 5,
        check_vma=False,
    )
```

time: 119 us -> 62.2 us (0.52)
  the two profiles are of different devices: /device:TPU:1 before, /device:TPU:12 now
where the time goes in v1:
time: 62.2 us; the launch traced here: 61.6 us
  Pallas kernels  48.9 us (79%)
  local copies, waits for them, and re-layouts  12 us (19%)
  between operations  0.66 us (1%)
    pallas_call x1, Pallas kernels, local(): pl.pallas_call(main_kernel, out_shape=(jax.ShapeDtypeStruct((2 * MINE, 2...  46.6 us
    unnamed x20, local copies, waits for them, and re-layouts  11.1 us
    pallas_call x1, Pallas kernels, local(): pl.pallas_call(place_kernel, out_shape=(field, field, field, flat, flat),...  2.4 us

profile of v1, /device:TPU:12, one launch (start us, length us, event | category | flops | bytes accessed | tf_op | source)
XLA Modules:
  0.0 61.6 jit_solution(4254258413506716609)
XLA Ops:
  0.6 0.8 %reshape.25 = s32[32,2,32]{2,1,0:T(2,128)S(1)} reshape(s32[32,64]{1,0:T(8,128)} %param.16) | data formatting | bytes 16384 | tf_op jit(solution)/shard_map/reshape | solution.py:317
  1.4 0.1 reshape.26.lab
  1.5 0.0 copy-start
  1.5 1.6 %copy-done = bf16[1,1024,1024]{2,1,0:T(8,128)(2,1)S(1)} copy-done((bf16[1,1024,1024]{2,1,0:T(8,128)(2,1)S(1)}, bf16[1,1024,1024]{2,1,0:T(8,128)(2,1)}, u32[]{:S(2)}) %copy-start) | copy-done | bytes 2097176
  3.1 0.0 copy-start.1
  3.1 1.6 %copy-done.1 = bf16[1,1024,1024]{2,1,0:T(8,128)(2,1)S(1)} copy-done((bf16[1,1024,1024]{2,1,0:T(8,128)(2,1)S(1)}, bf16[1,1024,1024]{2,1,0:T(8,128)(2,1)}, u32[]{:S(2)}) %copy-start.1) | copy-done | bytes 2097176
  4.7 0.0 copy-start.2
  4.7 1.0 %copy-done.2 = bf16[32,64,128]{2,1,0:T(8,128)(2,1)S(1)} copy-done((bf16[32,64,128]{2,1,0:T(8,128)(2,1)S(1)}, bf16[32,64,128]{2,1,0:T(8,128)(2,1)}, u32[]{:S(2)}) %copy-start.2) | copy-done | bytes 524312
  5.7 0.0 copy-start.3
  5.8 1.0 %copy-done.3 = bf16[32,64,128]{2,1,0:T(8,128)(2,1)S(1)} copy-done((bf16[32,64,128]{2,1,0:T(8,128)(2,1)S(1)}, bf16[32,64,128]{2,1,0:T(8,128)(2,1)}, u32[]{:S(2)}) %copy-start.3) | copy-done | bytes 524312
  6.8 0.0 copy-start.4
  6.8 1.0 %copy-done.4 = bf16[32,64,128]{2,1,0:T(8,128)(2,1)S(1)} copy-done((bf16[32,64,128]{2,1,0:T(8,128)(2,1)S(1)}, bf16[32,64,128]{2,1,0:T(8,128)(2,1)}, u32[]{:S(2)}) %copy-start.4) | copy-done | bytes 524312
  7.8 0.0 copy-start.5
  7.8 1.0 %copy-done.5 = bf16[32,64,128]{2,1,0:T(8,128)(2,1)S(1)} copy-done((bf16[32,64,128]{2,1,0:T(8,128)(2,1)S(1)}, bf16[32,64,128]{2,1,0:T(8,128)(2,1)}, u32[]{:S(2)}) %copy-start.5) | copy-done | bytes 524312
  8.9 0.0 copy-start.6
  8.9 1.0 %copy-done.6 = bf16[32,64,128]{2,1,0:T(8,128)(2,1)S(1)} copy-done((bf16[32,64,128]{2,1,0:T(8,128)(2,1)S(1)}, bf16[32,64,128]{2,1,0:T(8,128)(2,1)}, u32[]{:S(2)}) %copy-start.6) | copy-done | bytes 524312
  9.9 0.0 copy-start.7
  9.9 1.0 %copy-done.7 = bf16[1,256,1024]{2,1,0:T(8,128)(2,1)S(1)} copy-done((bf16[1,256,1024]{2,1,0:T(8,128)(2,1)S(1)}, bf16[1,256,1024]{2,1,0:T(8,128)(2,1)}, u32[]{:S(2)}) %copy-start.7) | copy-done | bytes 524312
  11.0 0.0 copy-start.8
  11.0 1.0 %copy-done.8 = bf16[1,1024,256]{2,1,0:T(8,128)(2,1)S(1)} copy-done((bf16[1,1024,256]{2,1,0:T(8,128)(2,1)S(1)}, bf16[1,1024,256]{2,1,0:T(8,128)(2,1)}, u32[]{:S(2)}) %copy-start.8) | copy-done | bytes 524312
  12.0 0.0 copy-start.9
  12.0 0.7 %copy-done.9 = f32[128]{0:T(128)S(1)} copy-done((f32[128]{0:T(128)S(1)}, f32[128]{0:T(128)}, u32[]{:S(2)}) %copy-start.9) | copy-done | bytes 536
  12.7 46.6 %main.1 = (bf16[2048,256]{1,0:T(8,128)(2,1)S(1)}, s32[16,128]{1,0:T(8,128)S(1)}, bf16[32,32,128]{2,1,0:T(8,128)(2,1)S(1)}, bf16[32,32,128]{2,1,0:T(8,128)(2,1)S(1)}, bf16[32,32,128]{2,1,0:T(8,128)(2,1)S(1)}) custom-call(s32[16,128]{1,0:T(8,128)S(1)} %reshape.26.lab, f32[1,128]{1,0:T(1,128)S(1)} %bitcast.6, bf16[32,64,128]{2,1,0:T(8,128)(2,1)S(1)} %copy-done.2, ...), custom_call_target="tpu_custom_call" | custom-call | tf_op jit(solution)/shard_map/main/pallas_call | solution.py:323
  59.2 2.4 %place.1 = (bf16[32,32,128]{2,1,0:T(8,128)(2,1)}, bf16[32,32,128]{2,1,0:T(8,128)(2,1)}, bf16[32,32,128]{2,1,0:T(8,128)(2,1)}, bf16[1024,128]{1,0:T(8,128)(2,1)}, bf16[1024,128]{1,0:T(8,128)(2,1)}) custom-call(s32[16,128]{1,0:T(8,128)S(1)} %get-tuple-element.15.slots, bf16[2048,256]{1,0:T(8,128)(2,1)S(1)} %get-tuple-element.16.back, ...), custom_call_target="tpu_custom_call" | custom-call | tf_op jit(solution)/shard_map/place/pallas_call | solution.py:363
  (1 shorter events, 0.0 us)
Async XLA Ops:
  1.5 1.6 %copy-start = (bf16[1,1024,1024]{2,1,0:T(8,128)(2,1)S(1)}, bf16[1,1024,1024]{2,1,0:T(8,128)(2,1)}, u32[]{:S(2)}) copy-start(bf16[1,1024,1024]{2,1,0:T(8,128)(2,1)} %w2h.1) | copy-start | bytes 6291460
  3.1 1.6 %copy-start.1 = (bf16[1,1024,1024]{2,1,0:T(8,128)(2,1)S(1)}, bf16[1,1024,1024]{2,1,0:T(8,128)(2,1)}, u32[]{:S(2)}) copy-start(bf16[1,1024,1024]{2,1,0:T(8,128)(2,1)} %w3h.1) | copy-start | bytes 6291460
  4.7 1.0 %copy-start.2 = (bf16[32,64,128]{2,1,0:T(8,128)(2,1)S(1)}, bf16[32,64,128]{2,1,0:T(8,128)(2,1)}, u32[]{:S(2)}) copy-start(bf16[32,64,128]{2,1,0:T(8,128)(2,1)} %therm.1) | copy-start | bytes 1572868
  5.7 1.0 %copy-start.3 = (bf16[32,64,128]{2,1,0:T(8,128)(2,1)S(1)}, bf16[32,64,128]{2,1,0:T(8,128)(2,1)}, u32[]{:S(2)}) copy-start(bf16[32,64,128]{2,1,0:T(8,128)(2,1)} %moist.1) | copy-start | bytes 1572868
  6.8 1.0 %copy-start.4 = (bf16[32,64,128]{2,1,0:T(8,128)(2,1)S(1)}, bf16[32,64,128]{2,1,0:T(8,128)(2,1)}, u32[]{:S(2)}) copy-start(bf16[32,64,128]{2,1,0:T(8,128)(2,1)} %zonal.1) | copy-start | bytes 1572868
  7.8 1.0 %copy-start.5 = (bf16[32,64,128]{2,1,0:T(8,128)(2,1)S(1)}, bf16[32,64,128]{2,1,0:T(8,128)(2,1)}, u32[]{:S(2)}) copy-start(bf16[32,64,128]{2,1,0:T(8,128)(2,1)} %merid.1) | copy-start | bytes 1572868
  8.9 1.0 %copy-start.6 = (bf16[32,64,128]{2,1,0:T(8,128)(2,1)S(1)}, bf16[32,64,128]{2,1,0:T(8,128)(2,1)}, u32[]{:S(2)}) copy-start(bf16[32,64,128]{2,1,0:T(8,128)(2,1)} %baro.1) | copy-start | bytes 1572868
  9.9 1.0 %copy-start.7 = (bf16[1,256,1024]{2,1,0:T(8,128)(2,1)S(1)}, bf16[1,256,1024]{2,1,0:T(8,128)(2,1)}, u32[]{:S(2)}) copy-start(bf16[1,256,1024]{2,1,0:T(8,128)(2,1)} %w1h.1) | copy-start | bytes 1572868
  11.0 1.0 %copy-start.8 = (bf16[1,1024,256]{2,1,0:T(8,128)(2,1)S(1)}, bf16[1,1024,256]{2,1,0:T(8,128)(2,1)}, u32[]{:S(2)}) copy-start(bf16[1,1024,256]{2,1,0:T(8,128)(2,1)} %w4h.1) | copy-start | bytes 1572868
  12.0 0.7 %copy-start.9 = (f32[128]{0:T(128)S(1)}, f32[128]{0:T(128)}, u32[]{:S(2)}) copy-start(f32[128]{0:T(128)} %param.17) | copy-start | bytes 1540

commit v2 on v1

--- a/solution.py
+++ b/solution.py
@@ -27,22 +27,48 @@
     return half * jnp.tanh(half) + half
 
 
-def offset(o):
-    dy = (o // 4) % 4
-    return dy, (o // 2) % 2, (o // 16 - dy + 4) % 4, o % 2
-
-
-def peer(o, sign, g, b):
-    dy, dx, dz, dc = offset(o)
-    y = (b // 16 + sign * dy + 4) % 4
-    x = (b // 8 + dx) % 2
-    z = ((b // 2) % 4 + sign * dz + 4) % 4
-    c = (b + dc) % 2
-    return {"grp": (g + dx) % 2, "blk": ((y * 2 + x) * 4 + z) * 2 + c}
+def span(steps):
+    dy, dx, dz, dc = steps
+    return min(dy, 4 - dy) + min(dz, 4 - dz) + dx + dc * 0.25
+
+
+def ordered():
+    near = sorted(
+        ((dy, dx, dz, dc) for dy in range(4) for dx in range(2) for dz in range(4) for dc in range(2)),
+        key=span,
+    )
+    return near[:PER] + near[PER:][::-1]
+
+
+ORDER = ordered()
+
+
+def peers(sign, g, b):
+    ys = [(b // 16 + sign * d + 4) % 4 * 16 for d in range(4)]
+    xs = [(b // 8 + d) % 2 * 8 for d in range(2)]
+    zs = [((b // 2) % 4 + sign * d + 4) % 4 * 2 for d in range(4)]
+    cs = [(b + d) % 2 for d in range(2)]
+    gs = [g, (g + 1) % 2]
+    out = []
+    for dy, dx, dz, dc in ORDER:
+        out.append({"grp": gs[dx], "blk": ys[dy] + xs[dx] + zs[dz] + cs[dc]})
+    return out
+
+
+def table_of(lab):
+    lane = lax.broadcasted_iota(jnp.int32, (8, 128), 1)
+    rows = [jnp.zeros((8, 128), jnp.int32) for _ in range(2)]
+    for q in range(4):
+        part = lab[pl.ds(q, 8, stride=4), :]
+        wide = jnp.concatenate([part, part], axis=1)
+        for h in range(2):
+            moved = pltpu.roll(wide, (q - h) % 4 * HALF, 1) if q != h else wide
+            rows[h] = jnp.where(lane // HALF == q, moved, rows[h])
+    return jnp.concatenate(rows, axis=0)
 
 
 def slots_of(lab, ot, cum, rank, g, b):
-    labels = lab[...]
+    labels = table_of(lab)
     sub = lax.broadcasted_iota(jnp.int32, (64, 128), 0)
     for k in range(16):
         hit = jnp.where(labels[k : k + 1, :] == sub, 1.0, 0.0)
@@ -62,7 +88,10 @@
     dx = ((labels >> 3) + b // 8) & 1
     dz = ((labels >> 1) - (b // 2) % 4 + 4) & 3
     dc = (labels + b) & 1
-    o = ((dy + dz) & 3) * 16 + dy * 4 + dx * 2 + dc
+    code = ((dy * 2 + dx) * 4 + dz) * 2 + dc
+    o = jnp.zeros_like(code)
+    for n, (oy, ox, oz, oc) in enumerate(ORDER):
+        o = jnp.where(code == ((oy * 2 + ox) * 4 + oz) * 2 + oc, n, o)
     side = ((place >> 4) + g + dx) & 1
     return side * MINE + o * PIECE + (place & (PIECE - 1))
 
@@ -98,16 +127,25 @@
 
 def main_kernel(
     lab, rate, therm, moist, zonal, merid, baro, w1h, w2h, w3h, w4h,
-    back, slots, east_o, north_o, press_o,
-    prof, pbuf, ot, cum, rank, send, recv, res, hid_a, hid_b, mine, theirs,
+    east_o, north_o, press_o, heat_o, moist_o,
+    slots, back, goal, prof, pbuf, ot, cum, rank, send, recv, res, hid_a, hid_b,
     w1, w2, w3, w4, stage, east, north, press,
-    load_sem, weight_sem, out_sem, fs_sem, fr_sem, rs_sem, rr_sem, ps_sem, pr_sem, hs_sem, hr_sem,
+    load_sem, weight_sem, fs_sem, fr_sem, rs_sem, rr_sem, ps_sem, pr_sem, hs_sem, hr_sem,
 ):
     g = lax.axis_index("grp")
     b = lax.axis_index("blk")
+    mine, theirs = back.at[pl.ds(0, MINE)], back.at[pl.ds(MINE, MINE)]
     partner = {"grp": (g + 1) % 2, "blk": b}
     right = {"grp": g, "blk": (b + 1) % 64}
     left = {"grp": g, "blk": (b + 63) % 64}
+
+    ahead, behind = peers(1, g, b), peers(-1, g, b)
+    barrier = pltpu.get_barrier_semaphore()
+
+    for o in reversed(range(1, PEERS)):
+        pl.semaphore_signal(barrier, inc=1, device_id=ahead[o], device_id_type=MESH)
+    for other in (partner, left, right):
+        pl.semaphore_signal(barrier, inc=1, device_id=other, device_id_type=MESH)
 
     loads = []
     for h in range(2):
@@ -136,16 +174,6 @@
     for copy in loads + fields + weights:
         copy.start()
 
-    barrier = pltpu.get_barrier_semaphore()
-
-    def greet(o, carry):
-        pl.semaphore_signal(barrier, inc=1, device_id=peer(o, 1, g, b), device_id_type=MESH)
-        return carry
-
-    lax.fori_loop(1, PEERS, greet, 0)
-    for other in (partner, left, right):
-        pl.semaphore_signal(barrier, inc=1, device_id=other, device_id_type=MESH)
-
     slot = slots_of(lab, ot, cum, rank, g, b)
     slots[...] = slot
     for copy in loads:
@@ -165,7 +193,7 @@
     pl.semaphore_wait(barrier, PEERS - 1 + 3)
 
     def piece(o):
-        return pl.ds(pl.multiple_of(o * PIECE, PIECE), PIECE)
+        return pl.ds(o * PIECE, PIECE)
 
     def forth(o):
         return pltpu.make_async_remote_copy(
@@ -173,7 +201,7 @@
             dst_ref=recv.at[piece(o)],
             send_sem=fs_sem.at[o],
             recv_sem=fr_sem.at[o],
-            device_id=peer(o, 1, g, b),
+            device_id=ahead[o],
             device_id_type=MESH,
         )
 
@@ -183,12 +211,12 @@
             dst_ref=mine.at[piece(o)],
             send_sem=rs_sem.at[o],
             recv_sem=rr_sem.at[o],
-            device_id=peer(o, -1, g, b),
+            device_id=behind[o],
             device_id_type=MESH,
         )
 
     def across(k):
-        rows = pl.ds(pl.multiple_of(k * CROWS, CROWS), CROWS)
+        rows = pl.ds(k * CROWS, CROWS)
         return pltpu.make_async_remote_copy(
             src_ref=mine.at[rows],
             dst_ref=theirs.at[rows],
@@ -199,11 +227,8 @@
         )
 
     def each(first, last, act):
-        def body(o, carry):
+        for o in range(first, last):
             act(o)
-            return carry
-
-        lax.fori_loop(first, last, body, 0)
 
     each(1, PEERS, lambda o: forth(o).start())
     for copy in fields:
@@ -221,15 +246,21 @@
     ]
     for copy in halos:
         copy.start()
+    places = slots[pl.ds(pl.multiple_of(g * 8, 8), 8), :].astype(F32)
+    columns = jnp.transpose(places).astype(jnp.int32)
+    lane = lax.broadcasted_iota(jnp.int32, (128, 2 * MINE), 1)
+    for k in range(8):
+        hit = jnp.where(columns[:, k : k + 1] == lane, 1.0, 0.0)
+        goal[k * 128 : (k + 1) * 128, :] = hit.astype(BF)
     for copy in weights:
         copy.wait()
 
     def hand_on(k):
-        each(jnp.maximum(k * PER, 1), (k + 1) * PER, lambda o: home(o).wait_recv())
+        each(max(k * PER, 1), (k + 1) * PER, lambda o: home(o).wait_recv())
         across(k).start()
 
     def network(k):
-        rows = pl.ds(pl.multiple_of(k * CROWS, CROWS), CROWS)
+        rows = pl.ds(k * CROWS, CROWS)
         x = recv[rows, :]
         for n in range(4):
             cut = slice(n * 256, (n + 1) * 256)
@@ -242,23 +273,15 @@
             hid_a[:, cut] = silu(jnp.dot(hid_b[...], w3[:, cut], preferred_element_type=F32)).astype(BF)
         res[rows, :] = jnp.dot(hid_a[...], w4[...], preferred_element_type=F32).astype(BF)
 
-    def turn(k, carry):
-        each(jnp.maximum(k * PER, 1), (k + 1) * PER, lambda o: forth(o).wait_recv())
+    for k in range(CHUNKS):
+        each(max(k * PER, 1), (k + 1) * PER, lambda o: forth(o).wait_recv())
         network(k)
-        each(jnp.maximum(k * PER, 1), (k + 1) * PER, lambda o: home(o).start())
-
-        @pl.when(k == 0)
-        def _():
+        each(max(k * PER, 1), (k + 1) * PER, lambda o: home(o).start())
+        if k == 0:
             mine[0:PIECE, :] = res[0:PIECE, :]
 
-        @pl.when(k >= 1)
-        def _():
-            hand_on(k - 1)
-
-        return carry
-
-    lax.fori_loop(0, CHUNKS, turn, 0)
-
+    for k in range(CHUNKS):
+        hand_on(k)
     for copy in halos:
         copy.wait()
 
@@ -269,9 +292,7 @@
         return carry
 
     lax.fori_loop(0, ROWS, widen, 0)
-    substep(0, rate, east, north, press)
-    hand_on(CHUNKS - 1)
-    for s in range(1, SUB):
+    for s in range(SUB):
         substep(s, rate, east, north, press)
     own = pl.ds(pl.multiple_of(g * HALO, 8), HALF)
 
@@ -283,53 +304,49 @@
 
     lax.fori_loop(0, CX, narrow, 0)
 
-    each(0, CHUNKS, lambda k: across(k).wait_send())
-    out_mine = pltpu.make_async_copy(mine, back.at[pl.ds(0, MINE)], out_sem.at[0])
-    out_mine.start()
-    each(0, CHUNKS, lambda k: across(k).wait_recv())
-    out_theirs = pltpu.make_async_copy(theirs, back.at[pl.ds(MINE, MINE)], out_sem.at[1])
-    out_theirs.start()
+    each(0, CHUNKS, lambda k: across(k).wait())
+    for k in range(4):
+        cut = slice(k * 256, (k + 1) * 256)
+        rows = jnp.dot(goal[cut, :], back[...], preferred_element_type=F32)
+        heat_o[cut, :] = rows[:, :LEV].astype(BF)
+        moist_o[cut, :] = rows[:, LEV:].astype(BF)
     each(1, PEERS, lambda o: forth(o).wait_send())
     each(1, PEERS, lambda o: home(o).wait_send())
-    out_mine.wait()
-    out_theirs.wait()
-
-
-def place_kernel(slots, back, east, north, press, east_o, north_o, press_o, heat, moist):
-    g = lax.axis_index("grp")
-    own = slots[pl.ds(pl.multiple_of(g * 8, 8), 8), :].astype(F32)
-    columns = jnp.transpose(own).astype(jnp.int32)
-    lane = lax.broadcasted_iota(jnp.int32, (128, 2 * MINE), 1)
-    for k in range(4):
-        hits = [
-            jnp.where(columns[:, 2 * k + q : 2 * k + q + 1] == lane, 1.0, 0.0).astype(BF)
-            for q in range(2)
-        ]
-        rows = jnp.dot(jnp.concatenate(hits, axis=0), back[...], preferred_element_type=F32)
-        heat[k * 256 : (k + 1) * 256, :] = rows[:, :LEV].astype(BF)
-        moist[k * 256 : (k + 1) * 256, :] = rows[:, LEV:].astype(BF)
-    east_o[...] = east[...]
-    north_o[...] = north[...]
-    press_o[...] = press[...]
+
+
+def store_kernel(*refs):
+    sources, targets, sem = refs[:5], refs[5:10], refs[10]
+    copies = [
+        pltpu.make_async_copy(src, dst, sem.at[n])
+        for n, (src, dst) in enumerate(zip(sources, targets))
+    ]
+    for copy in copies:
+        copy.start()
+    for copy in copies:
+        copy.wait()
 
 
 def local(zonal, merid, baro, therm, moist, labels, rate, w1, w2, w3, w4):
-    lab = labels.reshape(CX, 2, HALF).transpose(1, 0, 2).reshape(16, 128)
     vmem = pl.BlockSpec(memory_space=pltpu.VMEM)
-    hbm = pl.BlockSpec(memory_space=pl.ANY)
+    hbm = pl.BlockSpec(memory_space=pltpu.HBM)
     field = jax.ShapeDtypeStruct((CX, HALF, LEV), BF)
     dma = pltpu.SemaphoreType.DMA
     hid = w2.shape[-1]
-    back, slots, east, north, press = pl.pallas_call(
+    flat = jax.ShapeDtypeStruct((CX * HALF, LEV), BF)
+    kinds = (field, field, field, flat, flat)
+    inputs = [
+        pltpu.with_memory_space_constraint(a, pltpu.HBM)
+        for a in (labels, rate.reshape(1, LEV), therm, moist, zonal, merid, baro, w1, w2, w3, w4)
+    ]
+    results = pl.pallas_call(
         main_kernel,
-        out_shape=(
-            jax.ShapeDtypeStruct((2 * MINE, 2 * LEV), BF),
-            jax.ShapeDtypeStruct((16, 128), jnp.int32),
-            field, field, field,
-        ),
+        out_shape=kinds,
         in_specs=[vmem, vmem] + [hbm] * 9,
-        out_specs=(hbm, vmem, vmem, vmem, vmem),
+        out_specs=(vmem,) * 5,
         scratch_shapes=[
+            pltpu.VMEM((16, 128), jnp.int32),
+            pltpu.VMEM((2 * MINE, 2 * LEV), BF),
+            pltpu.VMEM((CX * HALF, 2 * MINE), BF),
             pltpu.VMEM((2, CX, HALF, 2 * LEV), BF),
             pltpu.VMEM((CROWS, COLS), BF),
             pltpu.VMEM((1024, 128), BF),
@@ -340,8 +357,6 @@
             pltpu.VMEM((MINE, 2 * LEV), BF),
             pltpu.VMEM((CROWS, hid), BF),
             pltpu.VMEM((CROWS, hid), BF),
-            pltpu.VMEM((MINE, 2 * LEV), BF),
-            pltpu.VMEM((MINE, 2 * LEV), BF),
             pltpu.VMEM(w1.shape[1:], BF),
             pltpu.VMEM(w2.shape[1:], BF),
             pltpu.VMEM(w3.shape[1:], BF),
@@ -350,7 +365,7 @@
             pltpu.VMEM((ROWS, WJ, LEV), F32),
             pltpu.VMEM((ROWS, WJ, LEV), F32),
             pltpu.VMEM((ROWS, WJ, LEV), F32),
-            dma((7,)), dma((4,)), dma((2,)),
+            dma((7,)), dma((4,)),
             dma((PEERS,)), dma((PEERS,)), dma((PEERS,)), dma((PEERS,)),
             dma((CHUNKS,)), dma((CHUNKS,)), dma((2,)), dma((2,)),
         ],
@@ -358,16 +373,16 @@
             collective_id=0, has_side_effects=True, vmem_limit_bytes=40 * 1024 * 1024
         ),
         name="main",
-    )(lab, rate.reshape(1, LEV), therm, moist, zonal, merid, baro, w1, w2, w3, w4)
-    flat = jax.ShapeDtypeStruct((CX * HALF, LEV), BF)
+    )(*inputs)
     east, north, press, heat, moistening = pl.pallas_call(
-        place_kernel,
-        out_shape=(field, field, field, flat, flat),
+        store_kernel,
+        out_shape=kinds,
         in_specs=[vmem] * 5,
-        out_specs=(vmem,) * 5,
-        compiler_params=pltpu.CompilerParams(vmem_limit_bytes=32 * 1024 * 1024),
-        name="place",
-    )(slots, back, east, north, press)
+        out_specs=(hbm,) * 5,
+        scratch_shapes=[dma((5,))],
+        compiler_params=pltpu.CompilerParams(vmem_limit_bytes=4 * 1024 * 1024),
+        name="store",
+    )(*results)
     return east, north, press, heat.reshape(CX, HALF, LEV), moistening.reshape(CX, HALF, LEV)
 
 

time: 62.2 us -> 46 us (0.74)
  the two profiles are of different devices: /device:TPU:12 before, /device:TPU:1 now
where the time goes in v2:
time: 46 us; the launch traced here: 45.8 us
  Pallas kernels  45.2 us (98%)
  between operations  0.64 us (1%)
    pallas_call x1, Pallas kernels, local(): pl.pallas_call(main_kernel, out_shape=kinds, in_specs=[vmem, vmem] + [hbm...  44.1 us
    pallas_call x1, Pallas kernels, local(): pl.pallas_call(store_kernel, out_shape=kinds, in_specs=[vmem] * 5, out_sp...  1.09 us

profile of v2, /device:TPU:1, one launch (start us, length us, event | category | flops | bytes accessed | tf_op | source)
XLA Modules:
  0.0 45.8 jit_solution(18128413068865789852)
XLA Ops:
  0.6 44.1 %main.1 = (bf16[32,32,128]{2,1,0:T(8,128)(2,1)S(1)}, bf16[32,32,128]{2,1,0:T(8,128)(2,1)S(1)}, bf16[32,32,128]{2,1,0:T(8,128)(2,1)S(1)}, bf16[1024,128]{1,0:T(8,128)(2,1)S(1)}, bf16[1024,128]{1,0:T(8,128)(2,1)S(1)}) custom-call(s32[32,64]{1,0:T(8,128)} %lab.1, f32[1,128]{1,0:T(1,128)} %bitcast.3, bf16[32,64,128]{2,1,0:T(8,128)(2,1)} %therm.1, ...), custom_call_target="tpu_custom_call" | custom-call | tf_op jit(solution)/shard_map/main/pallas_call | solution.py:341
  44.7 1.1 %store.1 = (bf16[32,32,128]{2,1,0:T(8,128)(2,1)}, bf16[32,32,128]{2,1,0:T(8,128)(2,1)}, bf16[32,32,128]{2,1,0:T(8,128)(2,1)}, bf16[1024,128]{1,0:T(8,128)(2,1)}, bf16[1024,128]{1,0:T(8,128)(2,1)}) custom-call(bf16[32,32,128]{2,1,0:T(8,128)(2,1)S(1)} %get-tuple-element.15.refs_0_, bf16[32,32,128]{2,1,0:T(8,128)(2,1)S(1)} %get-tuple-element.16.refs_1_, ...), custom_call_target="tpu_custom_call" | custom-call | tf_op jit(solution)/shard_map/store/pallas_call | solution.py:377

commit v3 on v2

--- a/solution.py
+++ b/solution.py
@@ -19,6 +19,13 @@
 CHUNKS = 4
 PER = PEERS // CHUNKS
 CROWS = PER * PIECE
+HANDS = 8
+HPER = PEERS // HANDS
+HROWS = HPER * PIECE
+HALO_TURN = 3
+DYN_AT = 8
+DIRECT = 16
+FIRST, LAST = DIRECT // HPER, (PEERS - PER) // HPER
 BF, F32 = jnp.bfloat16, jnp.float32
 
 
@@ -32,15 +39,10 @@
     return min(dy, 4 - dy) + min(dz, 4 - dz) + dx + dc * 0.25
 
 
-def ordered():
-    near = sorted(
-        ((dy, dx, dz, dc) for dy in range(4) for dx in range(2) for dz in range(4) for dc in range(2)),
-        key=span,
-    )
-    return near[:PER] + near[PER:][::-1]
-
-
-ORDER = ordered()
+ORDER = sorted(
+    ((dy, dx, dz, dc) for dy in range(4) for dx in range(2) for dz in range(4) for dc in range(2)),
+    key=span,
+)
 
 
 def peers(sign, g, b):
@@ -126,11 +128,11 @@
 
 
 def main_kernel(
-    lab, rate, therm, moist, zonal, merid, baro, w1h, w2h, w3h, w4h,
+    lab_h, rate_h, therm, moist, zonal, merid, baro, w1h, w2h, w3h, w4h,
     east_o, north_o, press_o, heat_o, moist_o,
-    slots, back, goal, prof, pbuf, ot, cum, rank, send, recv, res, hid_a, hid_b,
+    lab, rate, slots, back, goal, acc, prof, ot, cum, rank, send, recv, res, hid_a, hid_b,
     w1, w2, w3, w4, stage, east, north, press,
-    load_sem, weight_sem, fs_sem, fr_sem, rs_sem, rr_sem, ps_sem, pr_sem, hs_sem, hr_sem,
+    table_sem, load_sem, weight_sem, ds_sem, dr_sem, fs_sem, fr_sem, rs_sem, rr_sem, ps_sem, pr_sem, hs_sem, hr_sem,
 ):
     g = lax.axis_index("grp")
     b = lax.axis_index("blk")
@@ -140,13 +142,20 @@
     left = {"grp": g, "blk": (b + 63) % 64}
 
     ahead, behind = peers(1, g, b), peers(-1, g, b)
+    ahead_too, behind_too = [
+        [{"grp": (p["grp"] + 1) % 2, "blk": p["blk"]} for p in near[:DIRECT]] for near in (ahead, behind)
+    ]
     barrier = pltpu.get_barrier_semaphore()
 
     for o in reversed(range(1, PEERS)):
         pl.semaphore_signal(barrier, inc=1, device_id=ahead[o], device_id_type=MESH)
-    for other in (partner, left, right):
+    for other in ahead_too + [left, right]:
         pl.semaphore_signal(barrier, inc=1, device_id=other, device_id_type=MESH)
 
+    tables = [
+        pltpu.make_async_copy(src, dst, table_sem.at[n])
+        for n, (src, dst) in enumerate(((lab_h, lab), (rate_h, rate)))
+    ]
     loads = []
     for h in range(2):
         for f, src in enumerate((therm, moist)):
@@ -171,26 +180,26 @@
         pltpu.make_async_copy(src.at[0], dst, weight_sem.at[n])
         for n, (src, dst) in enumerate(((w1h, w1), (w2h, w2), (w3h, w3), (w4h, w4)))
     ]
-    for copy in loads + fields + weights:
+    for copy in tables + loads + fields + weights:
         copy.start()
 
-    slot = slots_of(lab, ot, cum, rank, g, b)
-    slots[...] = slot
+    for copy in tables:
+        copy.wait()
+    slots[...] = slots_of(lab, ot, cum, rank, g, b)
     for copy in loads:
         copy.wait()
 
-    def gather(m, carry):
+    for m in range(CHUNKS):
         want = lax.broadcasted_iota(jnp.int32, (CROWS, 128), 0) + m * CROWS
-        for k in range(16):
-            hit = jnp.where(slots[k : k + 1, :] == want, 1.0, 0.0)
-            pbuf[:, k * 128 : (k + 1) * 128] = hit.astype(BF)
-        rows = jnp.dot(pbuf[...], prof[...].reshape(COLS, 2 * LEV), preferred_element_type=F32)
-        send[pl.ds(pl.multiple_of(m * CROWS, CROWS), CROWS), :] = rows.astype(BF)
-        return carry
-
-    lax.fori_loop(0, CHUNKS, gather, 0)
+        hits = [jnp.where(slots[k : k + 1, :] == want, 1.0, 0.0).astype(BF) for k in range(16)]
+        rows = jnp.dot(
+            jnp.concatenate(hits, axis=1),
+            prof[...].reshape(COLS, 2 * LEV),
+            preferred_element_type=F32,
+        )
+        send[m * CROWS : (m + 1) * CROWS, :] = rows.astype(BF)
     recv[0:PIECE, :] = send[0:PIECE, :]
-    pl.semaphore_wait(barrier, PEERS - 1 + 3)
+    pl.semaphore_wait(barrier, PEERS - 1 + DIRECT + 2)
 
     def piece(o):
         return pl.ds(o * PIECE, PIECE)
@@ -199,8 +208,8 @@
         return pltpu.make_async_remote_copy(
             src_ref=send.at[piece(o)],
             dst_ref=recv.at[piece(o)],
-            send_sem=fs_sem.at[o],
-            recv_sem=fr_sem.at[o],
+            send_sem=fs_sem,
+            recv_sem=fr_sem.at[o // PER],
             device_id=ahead[o],
             device_id_type=MESH,
         )
@@ -209,19 +218,40 @@
         return pltpu.make_async_remote_copy(
             src_ref=res.at[piece(o)],
             dst_ref=mine.at[piece(o)],
-            send_sem=rs_sem.at[o],
-            recv_sem=rr_sem.at[o],
+            send_sem=rs_sem,
+            recv_sem=rr_sem.at[o // HPER],
             device_id=behind[o],
             device_id_type=MESH,
         )
 
+    def direct(o):
+        return pltpu.make_async_remote_copy(
+            src_ref=res.at[piece(o)],
+            dst_ref=theirs.at[piece(o)],
+            send_sem=ds_sem,
+            recv_sem=dr_sem,
+            device_id=behind_too[o],
+            device_id_type=MESH,
+        )
+
+    def bulk(ref, first, last, send_sem, recv_sem):
+        rows = ref.at[pl.ds(first * PIECE, (last - first) * PIECE)]
+        return pltpu.make_async_remote_copy(
+            src_ref=rows,
+            dst_ref=rows,
+            send_sem=send_sem,
+            recv_sem=recv_sem,
+            device_id=partner,
+            device_id_type=MESH,
+        )
+
     def across(k):
-        rows = pl.ds(k * CROWS, CROWS)
+        rows = pl.ds(k * HROWS, HROWS)
         return pltpu.make_async_remote_copy(
             src_ref=mine.at[rows],
             dst_ref=theirs.at[rows],
-            send_sem=ps_sem.at[k],
-            recv_sem=pr_sem.at[k],
+            send_sem=ps_sem,
+            recv_sem=pr_sem.at[k // LAST],
             device_id=partner,
             device_id_type=MESH,
         )
@@ -244,8 +274,6 @@
         )
         for n, (src, dst, other) in enumerate(((CX, 0, right), (HALO, HALO + CX, left)))
     ]
-    for copy in halos:
-        copy.start()
     places = slots[pl.ds(pl.multiple_of(g * 8, 8), 8), :].astype(F32)
     columns = jnp.transpose(places).astype(jnp.int32)
     lane = lax.broadcasted_iota(jnp.int32, (128, 2 * MINE), 1)
@@ -256,7 +284,7 @@
         copy.wait()
 
     def hand_on(k):
-        each(max(k * PER, 1), (k + 1) * PER, lambda o: home(o).wait_recv())
+        bulk(mine, max(k * HPER, 1), (k + 1) * HPER, rs_sem, rr_sem.at[k]).wait_recv()
         across(k).start()
 
     def network(k):
@@ -274,16 +302,15 @@
         res[rows, :] = jnp.dot(hid_a[...], w4[...], preferred_element_type=F32).astype(BF)
 
     for k in range(CHUNKS):
-        each(max(k * PER, 1), (k + 1) * PER, lambda o: forth(o).wait_recv())
+        bulk(recv, max(k * PER, 1), (k + 1) * PER, fs_sem, fr_sem.at[k]).wait_recv()
+        if k == HALO_TURN:
+            for copy in halos:
+                copy.start()
         network(k)
         each(max(k * PER, 1), (k + 1) * PER, lambda o: home(o).start())
+        each(k * PER, min((k + 1) * PER, DIRECT), lambda o: direct(o).start())
         if k == 0:
             mine[0:PIECE, :] = res[0:PIECE, :]
-
-    for k in range(CHUNKS):
-        hand_on(k)
-    for copy in halos:
-        copy.wait()
 
     def widen(i, carry):
         east[i] = stage[0, i].astype(F32)
@@ -291,9 +318,6 @@
         press[i] = stage[2, i].astype(F32)
         return carry
 
-    lax.fori_loop(0, ROWS, widen, 0)
-    for s in range(SUB):
-        substep(s, rate, east, north, press)
     own = pl.ds(pl.multiple_of(g * HALO, 8), HALF)
 
     def narrow(i, carry):
@@ -302,16 +326,38 @@
         press_o[i] = press[i + HALO, own].astype(BF)
         return carry
 
-    lax.fori_loop(0, CX, narrow, 0)
-
-    each(0, CHUNKS, lambda k: across(k).wait())
+    def dynamics():
+        for copy in halos:
+            copy.wait()
+        lax.fori_loop(0, ROWS, widen, 0)
+        for s in range(SUB):
+            substep(s, rate, east, north, press)
+        lax.fori_loop(0, CX, narrow, 0)
+
+    for k in range(FIRST, HANDS):
+        if k == DYN_AT:
+            dynamics()
+        hand_on(k)
+    if DYN_AT == HANDS:
+        dynamics()
+    for k in range(FIRST):
+        bulk(mine, max(k * HPER, 1), (k + 1) * HPER, rs_sem, rr_sem.at[k]).wait_recv()
+    bulk(theirs, 0, DIRECT, ds_sem, dr_sem).wait_recv()
+    bulk(theirs, DIRECT, LAST * HPER, ps_sem, pr_sem.at[0]).wait_recv()
+    early = MINE + LAST * HROWS
     for k in range(4):
         cut = slice(k * 256, (k + 1) * 256)
-        rows = jnp.dot(goal[cut, :], back[...], preferred_element_type=F32)
+        acc[cut, :] = jnp.dot(goal[cut, :early], back[:early, :], preferred_element_type=F32)
+    bulk(theirs, LAST * HPER, PEERS, ps_sem, pr_sem.at[1]).wait_recv()
+    for k in range(4):
+        cut = slice(k * 256, (k + 1) * 256)
+        rows = acc[cut, :] + jnp.dot(goal[cut, early:], back[early:, :], preferred_element_type=F32)
         heat_o[cut, :] = rows[:, :LEV].astype(BF)
         moist_o[cut, :] = rows[:, LEV:].astype(BF)
-    each(1, PEERS, lambda o: forth(o).wait_send())
-    each(1, PEERS, lambda o: home(o).wait_send())
+    bulk(theirs, DIRECT, PEERS, ps_sem, pr_sem.at[0]).wait_send()
+    bulk(theirs, 0, DIRECT, ds_sem, dr_sem).wait_send()
+    bulk(send, 1, PEERS, fs_sem, fr_sem.at[0]).wait_send()
+    bulk(res, 1, PEERS, rs_sem, rr_sem.at[0]).wait_send()
 
 
 def store_kernel(*refs):
@@ -341,14 +387,16 @@
     results = pl.pallas_call(
         main_kernel,
         out_shape=kinds,
-        in_specs=[vmem, vmem] + [hbm] * 9,
+        in_specs=[hbm] * 11,
         out_specs=(vmem,) * 5,
         scratch_shapes=[
+            pltpu.VMEM((CX, 2 * HALF), jnp.int32),
+            pltpu.VMEM((1, LEV), F32),
             pltpu.VMEM((16, 128), jnp.int32),
             pltpu.VMEM((2 * MINE, 2 * LEV), BF),
             pltpu.VMEM((CX * HALF, 2 * MINE), BF),
+            pltpu.VMEM((CX * HALF, 2 * LEV), F32),
             pltpu.VMEM((2, CX, HALF, 2 * LEV), BF),
-            pltpu.VMEM((CROWS, COLS), BF),
             pltpu.VMEM((1024, 128), BF),
             pltpu.VMEM((1024, 256), F32),
             pltpu.VMEM((16, 128), F32),
@@ -365,9 +413,9 @@
             pltpu.VMEM((ROWS, WJ, LEV), F32),
             pltpu.VMEM((ROWS, WJ, LEV), F32),
             pltpu.VMEM((ROWS, WJ, LEV), F32),
-            dma((7,)), dma((4,)),
-            dma((PEERS,)), dma((PEERS,)), dma((PEERS,)), dma((PEERS,)),
-            dma((CHUNKS,)), dma((CHUNKS,)), dma((2,)), dma((2,)),
+            dma((2,)), dma((7,)), dma((4,)), dma, dma,
+            dma, dma((CHUNKS,)), dma, dma((HANDS,)),
+            dma, dma((2,)), dma((2,)), dma((2,)),
         ],
         compiler_params=pltpu.CompilerParams(
             collective_id=0, has_side_effects=True, vmem_limit_bytes=40 * 1024 * 1024

time: 46 us -> 37.6 us (0.82)
  Pallas kernels: 45.2 us -> 36.8 us
    pallas_call x1, Pallas kernels: 44.1 us -> 35.7 us  [local(): pl.pallas_call(main_kernel, out_shape=kinds, in_specs=[hbm] * 11, out_spe...]
where the time goes in v3:
time: 37.6 us; the launch traced here: 37.5 us
  Pallas kernels  36.8 us (98%)
  between operations  0.64 us (2%)
    pallas_call x1, Pallas kernels, local(): pl.pallas_call(main_kernel, out_shape=kinds, in_specs=[hbm] * 11, out_spe...  35.7 us
    pallas_call x1, Pallas kernels, local(): pl.pallas_call(store_kernel, out_shape=kinds, in_specs=[vmem] * 5, out_sp...  1.09 us

profile of v3, /device:TPU:1, one launch (start us, length us, event | category | flops | bytes accessed | tf_op | source)
XLA Modules:
  0.0 37.5 jit_solution(6685531426790716786)
XLA Ops:
  0.6 35.7 %main.1 = (bf16[32,32,128]{2,1,0:T(8,128)(2,1)S(1)}, bf16[32,32,128]{2,1,0:T(8,128)(2,1)S(1)}, bf16[32,32,128]{2,1,0:T(8,128)(2,1)S(1)}, bf16[1024,128]{1,0:T(8,128)(2,1)S(1)}, bf16[1024,128]{1,0:T(8,128)(2,1)S(1)}) custom-call(s32[32,64]{1,0:T(8,128)} %lab_h.1, f32[1,128]{1,0:T(1,128)} %bitcast.3, bf16[32,64,128]{2,1,0:T(8,128)(2,1)} %therm.1, ...), custom_call_target="tpu_custom_call" | custom-call | tf_op jit(solution)/shard_map/main/pallas_call | solution.py:387
  36.4 1.1 %store.1 = (bf16[32,32,128]{2,1,0:T(8,128)(2,1)}, bf16[32,32,128]{2,1,0:T(8,128)(2,1)}, bf16[32,32,128]{2,1,0:T(8,128)(2,1)}, bf16[1024,128]{1,0:T(8,128)(2,1)}, bf16[1024,128]{1,0:T(8,128)(2,1)}) custom-call(bf16[32,32,128]{2,1,0:T(8,128)(2,1)S(1)} %get-tuple-element.15.refs_0_, bf16[32,32,128]{2,1,0:T(8,128)(2,1)S(1)} %get-tuple-element.16.refs_1_, ...), custom_call_target="tpu_custom_call" | custom-call | tf_op jit(solution)/shard_map/store/pallas_call | solution.py:425

commit v4 on v3

--- a/solution.py
+++ b/solution.py
@@ -22,8 +22,6 @@
 HANDS = 8
 HPER = PEERS // HANDS
 HROWS = HPER * PIECE
-HALO_TURN = 3
-DYN_AT = 8
 DIRECT = 16
 FIRST, LAST = DIRECT // HPER, (PEERS - PER) // HPER
 BF, F32 = jnp.bfloat16, jnp.float32
@@ -105,26 +103,20 @@
     return up - down
 
 
-def substep(s, rate, east, north, press):
-    lo, hi = 2 * (s + 1), ROWS - 2 * (s + 1)
-    half = jnp.broadcast_to(rate[...] * 0.5, (WJ, LEV))
-    p_lo, p_next = press[lo], press[lo + 1]
-    e_before = east[lo - 1] - half * (p_lo - press[lo - 2])
-    e_here = east[lo] - half * (p_next - press[lo - 1])
-    east[lo - 1] = e_before
-    east[lo] = e_here
-
-    def step(i, carry):
-        e_before, e_here, p_here, p_next = carry
-        p_after = press[i + 2]
-        e_next = east[i + 1] - half * (p_after - p_here)
-        east[i + 1] = e_next
-        n_here = north[i] - half * slope(p_here)
-        north[i] = n_here
-        press[i] = p_here - half * ((e_next - e_before) + slope(n_here))
-        return e_here, e_next, p_next, p_after
-
-    lax.fori_loop(lo, hi, step, (e_before, e_here, p_lo, p_next))
+def advance(half, east, north, press, winds, cells):
+    def wind(i, carry):
+        east[i] = east[i] - half * (press[i + 1] - press[i - 1])
+        return carry
+
+    def cell(i, carry):
+        here = press[i]
+        wind_north = north[i] - half * slope(here)
+        north[i] = wind_north
+        press[i] = here - half * ((east[i + 1] - east[i - 1]) + slope(wind_north))
+        return carry
+
+    lax.fori_loop(*winds, wind, 0, unroll=2)
+    lax.fori_loop(*cells, cell, 0, unroll=2)
 
 
 def main_kernel(
@@ -145,13 +137,6 @@
     ahead_too, behind_too = [
         [{"grp": (p["grp"] + 1) % 2, "blk": p["blk"]} for p in near[:DIRECT]] for near in (ahead, behind)
     ]
-    barrier = pltpu.get_barrier_semaphore()
-
-    for o in reversed(range(1, PEERS)):
-        pl.semaphore_signal(barrier, inc=1, device_id=ahead[o], device_id_type=MESH)
-    for other in ahead_too + [left, right]:
-        pl.semaphore_signal(barrier, inc=1, device_id=other, device_id_type=MESH)
-
     tables = [
         pltpu.make_async_copy(src, dst, table_sem.at[n])
         for n, (src, dst) in enumerate(((lab_h, lab), (rate_h, rate)))
@@ -166,6 +151,16 @@
                     load_sem.at[2 * h + f],
                 )
             )
+    for copy in tables + loads:
+        copy.start()
+
+    barrier = pltpu.get_barrier_semaphore()
+
+    for o in reversed(range(1, PEERS)):
+        pl.semaphore_signal(barrier, inc=1, device_id=ahead[o], device_id_type=MESH)
+    for other in ahead_too + [left, right]:
+        pl.semaphore_signal(barrier, inc=1, device_id=other, device_id_type=MESH)
+
     fields = []
     window = pl.multiple_of(g * (HALF - HALO), 8)
     for f, src in enumerate((zonal, merid, baro)):
@@ -180,7 +175,7 @@
         pltpu.make_async_copy(src.at[0], dst, weight_sem.at[n])
         for n, (src, dst) in enumerate(((w1h, w1), (w2h, w2), (w3h, w3), (w4h, w4)))
     ]
-    for copy in tables + loads + fields + weights:
+    for copy in fields + weights:
         copy.start()
 
     for copy in tables:
@@ -261,8 +256,6 @@
             act(o)
 
     each(1, PEERS, lambda o: forth(o).start())
-    for copy in fields:
-        copy.wait()
     halos = [
         pltpu.make_async_remote_copy(
             src_ref=stage.at[:, pl.ds(src, HALO)],
@@ -280,6 +273,19 @@
     for k in range(8):
         hit = jnp.where(columns[:, k : k + 1] == lane, 1.0, 0.0)
         goal[k * 128 : (k + 1) * 128, :] = hit.astype(BF)
+    for copy in fields:
+        copy.wait()
+
+    def widen(i, carry):
+        east[i] = stage[0, i].astype(F32)
+        north[i] = stage[1, i].astype(F32)
+        press[i] = stage[2, i].astype(F32)
+        return carry
+
+    half = jnp.broadcast_to(rate[...] * 0.5, (WJ, LEV))
+    lax.fori_loop(HALO, HALO + CX, widen, 0)
+    for s in range(2, 2 * SUB + 2, 2):
+        advance(half, east, north, press, (s + 7, ROWS - 7 - s), (s + 8, ROWS - 8 - s))
     for copy in weights:
         copy.wait()
 
@@ -303,21 +309,12 @@
 
     for k in range(CHUNKS):
         bulk(recv, max(k * PER, 1), (k + 1) * PER, fs_sem, fr_sem.at[k]).wait_recv()
-        if k == HALO_TURN:
-            for copy in halos:
-                copy.start()
         network(k)
         each(max(k * PER, 1), (k + 1) * PER, lambda o: home(o).start())
         each(k * PER, min((k + 1) * PER, DIRECT), lambda o: direct(o).start())
         if k == 0:
             mine[0:PIECE, :] = res[0:PIECE, :]
 
-    def widen(i, carry):
-        east[i] = stage[0, i].astype(F32)
-        north[i] = stage[1, i].astype(F32)
-        press[i] = stage[2, i].astype(F32)
-        return carry
-
     own = pl.ds(pl.multiple_of(g * HALO, 8), HALF)
 
     def narrow(i, carry):
@@ -326,20 +323,18 @@
         press_o[i] = press[i + HALO, own].astype(BF)
         return carry
 
-    def dynamics():
-        for copy in halos:
-            copy.wait()
-        lax.fori_loop(0, ROWS, widen, 0)
-        for s in range(SUB):
-            substep(s, rate, east, north, press)
-        lax.fori_loop(0, CX, narrow, 0)
-
+    for copy in halos:
+        copy.start()
     for k in range(FIRST, HANDS):
-        if k == DYN_AT:
-            dynamics()
         hand_on(k)
-    if DYN_AT == HANDS:
-        dynamics()
+    for copy in halos:
+        copy.wait()
+    lax.fori_loop(0, HALO, widen, 0)
+    lax.fori_loop(HALO + CX, ROWS, widen, 0)
+    for s in range(2, 2 * SUB + 2, 2):
+        advance(half, east, north, press, (s - 1, s + 7), (s, s + 8))
+        advance(half, east, north, press, (ROWS - 7 - s, ROWS + 1 - s), (ROWS - 8 - s, ROWS - s))
+    lax.fori_loop(0, CX, narrow, 0)
     for k in range(FIRST):
         bulk(mine, max(k * HPER, 1), (k + 1) * HPER, rs_sem, rr_sem.at[k]).wait_recv()
     bulk(theirs, 0, DIRECT, ds_sem, dr_sem).wait_recv()

time: 37.6 us -> 36.3 us (0.965)
  Pallas kernels: 36.8 us -> 35.5 us
    pallas_call x1, Pallas kernels: 35.7 us -> 34.4 us  [local(): pl.pallas_call(main_kernel, out_shape=kinds, in_specs=[hbm] * 11, out_spe...]
where the time goes in v4:
time: 36.3 us; the launch traced here: 36.1 us
  Pallas kernels  35.5 us (98%)
  between operations  0.64 us (2%)
    pallas_call x1, Pallas kernels, local(): pl.pallas_call(main_kernel, out_shape=kinds, in_specs=[hbm] * 11, out_spe...  34.4 us
    pallas_call x1, Pallas kernels, local(): pl.pallas_call(store_kernel, out_shape=kinds, in_specs=[vmem] * 5, out_sp...  1.09 us

profile of v4, /device:TPU:1, one launch (start us, length us, event | category | flops | bytes accessed | tf_op | source)
XLA Modules:
  0.0 36.1 jit_solution(4442368152208924839)
XLA Ops:
  0.6 34.4 %main.1 = (bf16[32,32,128]{2,1,0:T(8,128)(2,1)S(1)}, bf16[32,32,128]{2,1,0:T(8,128)(2,1)S(1)}, bf16[32,32,128]{2,1,0:T(8,128)(2,1)S(1)}, bf16[1024,128]{1,0:T(8,128)(2,1)S(1)}, bf16[1024,128]{1,0:T(8,128)(2,1)S(1)}) custom-call(s32[32,64]{1,0:T(8,128)} %lab_h.1, f32[1,128]{1,0:T(1,128)} %bitcast.3, bf16[32,64,128]{2,1,0:T(8,128)(2,1)} %therm.1, ...), custom_call_target="tpu_custom_call" | custom-call | tf_op jit(solution)/shard_map/main/pallas_call | solution.py:382
  35.0 1.1 %store.1 = (bf16[32,32,128]{2,1,0:T(8,128)(2,1)}, bf16[32,32,128]{2,1,0:T(8,128)(2,1)}, bf16[32,32,128]{2,1,0:T(8,128)(2,1)}, bf16[1024,128]{1,0:T(8,128)(2,1)}, bf16[1024,128]{1,0:T(8,128)(2,1)}) custom-call(bf16[32,32,128]{2,1,0:T(8,128)(2,1)S(1)} %get-tuple-element.15.refs_0_, bf16[32,32,128]{2,1,0:T(8,128)(2,1)S(1)} %get-tuple-element.16.refs_1_, ...), custom_call_target="tpu_custom_call" | custom-call | tf_op jit(solution)/shard_map/store/pallas_call | solution.py:420

commit v5 on v4

--- a/solution.py
+++ b/solution.py
@@ -296,14 +296,14 @@
     def network(k):
         rows = pl.ds(k * CROWS, CROWS)
         x = recv[rows, :]
-        for n in range(4):
-            cut = slice(n * 256, (n + 1) * 256)
+        for n in range(2):
+            cut = slice(n * 512, (n + 1) * 512)
             hid_a[:, cut] = silu(jnp.dot(x, w1[:, cut], preferred_element_type=F32)).astype(BF)
-        for n in range(4):
-            cut = slice(n * 256, (n + 1) * 256)
+        for n in range(2):
+            cut = slice(n * 512, (n + 1) * 512)
             hid_b[:, cut] = silu(jnp.dot(hid_a[...], w2[:, cut], preferred_element_type=F32)).astype(BF)
-        for n in range(4):
-            cut = slice(n * 256, (n + 1) * 256)
+        for n in range(2):
+            cut = slice(n * 512, (n + 1) * 512)
             hid_a[:, cut] = silu(jnp.dot(hid_b[...], w3[:, cut], preferred_element_type=F32)).astype(BF)
         res[rows, :] = jnp.dot(hid_a[...], w4[...], preferred_element_type=F32).astype(BF)
 

time: 36.3 us -> 36.3 us (level)
  no operation moved by 1% of the time
where the time goes in v5:
time: 36.3 us; the launch traced here: 36.1 us
  Pallas kernels  35.5 us (98%)
  between operations  0.64 us (2%)
    pallas_call x1, Pallas kernels, local(): pl.pallas_call(main_kernel, out_shape=kinds, in_specs=[hbm] * 11, out_spe...  34.4 us
    pallas_call x1, Pallas kernels, local(): pl.pallas_call(store_kernel, out_shape=kinds, in_specs=[vmem] * 5, out_sp...  1.09 us

profile of v5, /device:TPU:1, one launch (start us, length us, event | category | flops | bytes accessed | tf_op | source)
XLA Modules:
  0.0 36.1 jit_solution(4442368152208924839)
XLA Ops:
  0.6 34.4 %main.1 = (bf16[32,32,128]{2,1,0:T(8,128)(2,1)S(1)}, bf16[32,32,128]{2,1,0:T(8,128)(2,1)S(1)}, bf16[32,32,128]{2,1,0:T(8,128)(2,1)S(1)}, bf16[1024,128]{1,0:T(8,128)(2,1)S(1)}, bf16[1024,128]{1,0:T(8,128)(2,1)S(1)}) custom-call(s32[32,64]{1,0:T(8,128)} %lab_h.1, f32[1,128]{1,0:T(1,128)} %bitcast.3, bf16[32,64,128]{2,1,0:T(8,128)(2,1)} %therm.1, ...), custom_call_target="tpu_custom_call" | custom-call | tf_op jit(solution)/shard_map/main/pallas_call | solution.py:382
  35.0 1.1 %store.1 = (bf16[32,32,128]{2,1,0:T(8,128)(2,1)}, bf16[32,32,128]{2,1,0:T(8,128)(2,1)}, bf16[32,32,128]{2,1,0:T(8,128)(2,1)}, bf16[1024,128]{1,0:T(8,128)(2,1)}, bf16[1024,128]{1,0:T(8,128)(2,1)}) custom-call(bf16[32,32,128]{2,1,0:T(8,128)(2,1)S(1)} %get-tuple-element.15.refs_0_, bf16[32,32,128]{2,1,0:T(8,128)(2,1)S(1)} %get-tuple-element.16.refs_1_, ...), custom_call_target="tpu_custom_call" | custom-call | tf_op jit(solution)/shard_map/store/pallas_call | solution.py:420
